TPU v7x, 16 devices: a 4x2x1 block of a 4x4x8 slice. The times are simulated.
16 devices in a mesh: dp: 2 (over y, z), tp: 8 (over x, core).
Axes of the slice: x: 4, y: 2, z: 1, core: 2. Of those that a mesh axis runs over, the one named last changes fastest.
The devices are a block of a 4x4x8 slice.
Arguments:
- x_in: float32 [16, 256, 2304], P('dp', 'tp'), parts along dimension 0
- d_out: bfloat16 [16, 256, 2304], P('dp', 'tp'), parts along dimension 0
- lengths: int32 [16], P('dp'), parts along dimension 0
- w_qkv: bfloat16 [3, 2304, 3, 24, 96], P(None, None, None, 'tp')
- w_out: bfloat16 [3, 24, 96, 2304], P(None, 'tp')
- w_up: bfloat16 [3, 2304, 9216], P(None, None, 'tp')
- b_up: float32 [3, 9216], P(None, 'tp')
- w_down: bfloat16 [3, 9216, 2304], P(None, 'tp')
- vec_par: float32 [3, 6, 2304], replicated
Outputs:
- output 1: float32 [16, 256, 2304], P('dp', 'tp'), parts along dimension 0
- output 2: float32 [16, 256, 2304], P('dp', 'tp'), parts along dimension 0
- output 3: bfloat16 [6, 2304, 3, 24, 96], P('dp', None, None, 'tp'), parts along dimension 0
- output 4: bfloat16 [6, 24, 96, 2304], P('dp', 'tp'), parts along dimension 0
- output 5: bfloat16 [6, 2304, 9216], P('dp', None, 'tp'), parts along dimension 0
- output 6: float32 [6, 9216], P('dp', 'tp'), parts along dimension 0
- output 7: bfloat16 [6, 9216, 2304], P('dp', 'tp'), parts along dimension 0
- output 8: float32 [6, 6, 2304], P('dp'), parts along dimension 0
There are 2 independent parts. A program takes and returns all parts, laid end to end along the dimension named above; an argument that names none is the same for every part.
All inputs are finite; a program needn't handle non-finite values.
Results may differ from a plain program's by a relative error of at most 0.02.
Values are sent between devices in bfloat16 or wider.
A program may use at most 768 MiB of HBM per device.

v0:
```python
import jax
import jax.numpy as jnp
from jax import lax
from jax.sharding import PartitionSpec as P

TENSOR_AXIS = 'tp'
PARTS_AXIS = 'dp'


def layer_norm(x_val, gain_vec, shift_vec):
    row_mean = jnp.mean(x_val, axis=-1, keepdims=True)
    centered = x_val - row_mean
    row_var = jnp.mean(centered * centered, axis=-1, keepdims=True)
    return centered * lax.rsqrt(row_var + 1e-5) * gain_vec + shift_vec


def gelu_tanh(pre_act):
    return jax.nn.gelu(pre_act, approximate=True)


def visible_mask(lengths, seq_len):
    positions = jnp.arange(seq_len)
    causal = positions[None, :] <= positions[:, None]
    return causal[None, None] & (positions[None, None, None, :] < lengths[:, None, None, None])


def attention_fwd(q_all, k_all, v_all, lengths):
    score_scale = q_all.shape[3] ** -0.5
    scores = jnp.einsum('bhqe,bhke->bhqk', q_all, k_all, preferred_element_type=jnp.float32) * score_scale
    attn_prob = jax.nn.softmax(jnp.where(visible_mask(lengths, q_all.shape[2]), scores, -1e30), axis=-1)
    context = jnp.einsum('bhqk,bhke->bhqe', attn_prob.astype(jnp.bfloat16), v_all, preferred_element_type=jnp.float32)
    return context.astype(jnp.bfloat16), attn_prob


def attention_bwd(d_ctx, q_all, k_all, v_all, attn_prob):
    score_scale = q_all.shape[3] ** -0.5
    d_prob = jnp.einsum('bhqe,bhke->bhqk', d_ctx, v_all, preferred_element_type=jnp.float32).astype(jnp.bfloat16).astype(jnp.float32)
    d_v = jnp.einsum('bhqk,bhqe->bhke', attn_prob.astype(jnp.bfloat16), d_ctx, preferred_element_type=jnp.float32).astype(jnp.bfloat16)
    d_score = attn_prob * (d_prob - jnp.sum(d_prob * attn_prob, axis=-1, keepdims=True))
    d_score = (d_score * score_scale).astype(jnp.bfloat16)
    d_q = jnp.einsum('bhqk,bhke->bhqe', d_score, k_all, preferred_element_type=jnp.float32).astype(jnp.bfloat16)
    d_k = jnp.einsum('bhqk,bhqe->bhke', d_score, q_all, preferred_element_type=jnp.float32).astype(jnp.bfloat16)
    return jnp.stack([d_q, d_k, d_v])


def layer_fwd(x_cur, lengths, weights, vec_layer):
    w_qkv, w_out, w_up, b_up, w_down = weights
    a_shard = layer_norm(x_cur, vec_layer[0], vec_layer[1]).astype(jnp.bfloat16)
    a_full = lax.all_gather(a_shard, TENSOR_AXIS, axis=1, tiled=True)
    qkv_all = jnp.einsum('bsd,dthe->tbhse', a_full, w_qkv, preferred_element_type=jnp.float32).astype(jnp.bfloat16)
    context, attn_prob = attention_fwd(qkv_all[0], qkv_all[1], qkv_all[2], lengths)
    attn_part = jnp.einsum('bhse,hed->bsd', context, w_out, preferred_element_type=jnp.float32).astype(jnp.bfloat16)
    attn_shard = lax.psum_scatter(attn_part, TENSOR_AXIS, scatter_dimension=1, tiled=True)
    hidden = x_cur + attn_shard.astype(jnp.float32) + vec_layer[4]
    m_shard = layer_norm(hidden, vec_layer[2], vec_layer[3]).astype(jnp.bfloat16)
    m_full = lax.all_gather(m_shard, TENSOR_AXIS, axis=1, tiled=True)
    pre_act = jnp.einsum('bsd,df->bsf', m_full, w_up, preferred_element_type=jnp.float32) + b_up
    act_bf = gelu_tanh(pre_act).astype(jnp.bfloat16)
    mlp_part = jnp.einsum('bsf,fd->bsd', act_bf, w_down, preferred_element_type=jnp.float32).astype(jnp.bfloat16)
    mlp_shard = lax.psum_scatter(mlp_part, TENSOR_AXIS, scatter_dimension=1, tiled=True)
    x_next = hidden + mlp_shard.astype(jnp.float32) + vec_layer[5]
    return x_next, (x_cur, a_full, qkv_all, context, attn_prob, hidden, m_full, pre_act, act_bf)


def layer_bwd(d_cur, residues, weights, vec_layer):
    w_qkv, w_out, w_up, w_down = weights[0], weights[1], weights[2], weights[4]
    x_prev, a_full, qkv_all, context, attn_prob, hidden, m_full, pre_act, act_bf = residues
    d_mlp = lax.all_gather(d_cur.astype(jnp.bfloat16), TENSOR_AXIS, axis=1, tiled=True)
    d_act = jnp.einsum('bsd,fd->bsf', d_mlp, w_down, preferred_element_type=jnp.float32).astype(jnp.bfloat16)
    g_down = jnp.einsum('bsf,bsd->fd', act_bf, d_mlp, preferred_element_type=jnp.float32).astype(jnp.bfloat16)
    d_pre = jax.vjp(gelu_tanh, pre_act)[1](d_act.astype(jnp.float32))[0]
    d_pre_bf = d_pre.astype(jnp.bfloat16)
    g_up = jnp.einsum('bsd,bsf->df', m_full, d_pre_bf, preferred_element_type=jnp.float32).astype(jnp.bfloat16)
    g_bup = jnp.sum(d_pre, axis=(0, 1))
    d_mid_part = jnp.einsum('bsf,df->bsd', d_pre_bf, w_up, preferred_element_type=jnp.float32).astype(jnp.bfloat16)
    d_mid = lax.psum_scatter(d_mid_part, TENSOR_AXIS, scatter_dimension=1, tiled=True)
    d_hid_ln, d_gain2, d_shift2 = jax.vjp(layer_norm, hidden, vec_layer[2], vec_layer[3])[1](d_mid.astype(jnp.float32))
    d_hid = d_cur + d_hid_ln
    d_attn = lax.all_gather(d_hid.astype(jnp.bfloat16), TENSOR_AXIS, axis=1, tiled=True)
    d_ctx = jnp.einsum('bsd,hed->bhse', d_attn, w_out, preferred_element_type=jnp.float32).astype(jnp.bfloat16)
    g_out = jnp.einsum('bhse,bsd->hed', context, d_attn, preferred_element_type=jnp.float32).astype(jnp.bfloat16)
    d_qkv = attention_bwd(d_ctx, qkv_all[0], qkv_all[1], qkv_all[2], attn_prob)
    g_qkv = jnp.einsum('bsd,tbhse->dthe', a_full, d_qkv, preferred_element_type=jnp.float32).astype(jnp.bfloat16)
    d_in_part = jnp.einsum('tbhse,dthe->bsd', d_qkv, w_qkv, preferred_element_type=jnp.float32).astype(jnp.bfloat16)
    d_in = lax.psum_scatter(d_in_part, TENSOR_AXIS, scatter_dimension=1, tiled=True)
    d_x_ln, d_gain1, d_shift1 = jax.vjp(layer_norm, x_prev, vec_layer[0], vec_layer[1])[1](d_in.astype(jnp.float32))
    g_vec = jnp.stack([d_gain1, d_shift1, d_gain2, d_shift2, jnp.sum(d_hid, axis=(0, 1)), jnp.sum(d_cur, axis=(0, 1))])
    return d_hid + d_x_ln, (g_qkv, g_out, g_up, g_bup, g_down, g_vec)


def group_body(x_loc, dy_loc, len_loc, wqkv_loc, wout_loc, wup_loc, bup_loc, wdown_loc, vec_loc):
    n_layers = wqkv_loc.shape[0]
    saved_acts = []
    x_cur = x_loc
    for layer_idx in range(n_layers):
        weights = (wqkv_loc[layer_idx], wout_loc[layer_idx], wup_loc[layer_idx], bup_loc[layer_idx], wdown_loc[layer_idx])
        x_cur, residues = layer_fwd(x_cur, len_loc, weights, vec_loc[layer_idx])
        saved_acts.append(residues)
    d_cur = dy_loc.astype(jnp.float32)
    layer_grads = [None] * n_layers
    for layer_idx in reversed(range(n_layers)):
        weights = (wqkv_loc[layer_idx], wout_loc[layer_idx], wup_loc[layer_idx], bup_loc[layer_idx], wdown_loc[layer_idx])
        d_cur, grad_set = layer_bwd(d_cur, saved_acts[layer_idx], weights, vec_loc[layer_idx])
        layer_grads[layer_idx] = grad_set
    stacked = [jnp.stack([grad_set[grad_pos] for grad_set in layer_grads]) for grad_pos in range(6)]
    g_vec = lax.psum(stacked[5], TENSOR_AXIS)
    return x_cur, d_cur, stacked[0], stacked[1], stacked[2], stacked[3], stacked[4], g_vec


def solution(mesh):
    act_spec = P(PARTS_AXIS, TENSOR_AXIS, None)
    in_specs = (act_spec, act_spec, P(PARTS_AXIS), P(None, None, None, TENSOR_AXIS, None), P(None, TENSOR_AXIS, None, None), P(None, None, TENSOR_AXIS), P(None, TENSOR_AXIS), P(None, TENSOR_AXIS, None), P())
    out_specs = (act_spec, act_spec, P(PARTS_AXIS, None, None, TENSOR_AXIS, None), P(PARTS_AXIS, TENSOR_AXIS, None, None), P(PARTS_AXIS, None, TENSOR_AXIS), P(PARTS_AXIS, TENSOR_AXIS), P(PARTS_AXIS, TENSOR_AXIS, None), P(PARTS_AXIS, None, None))
    return jax.shard_map(group_body, mesh=mesh, in_specs=in_specs, out_specs=out_specs, check_vma=False)
```

profile of v0, /device:TPU:113, one launch (start us, length us, event | category | flops | bytes accessed | tf_op | source)
XLA Modules:
  0.0 1871.8 jit_solution(5792880687835277922)
XLA Ops:
  13.8 52.7 %all-gather.13.cloned.1.call-done = bf16[8,256,2304]{2,1,0:T(8,128)(2,1)} async-done(((bf16[8,32,2304]{2,1,0:T(8,128)(2,1)}), bf16[8,256,2304]{2,1,0:T(8,128)(2,1)}) %all-gather.13.cloned.1.call-update) | async-done | bytes 9437200 | tf_op jit(solution)/shard_map/all_gather | solution.py:49
  95.1 52.9 %reduce-scatter.13.cloned.1.call-done = bf16[8,32,2304]{2,1,0:T(8,128)(2,1)} async-done(((bf16[8,256,2304]{2,1,0:T(8,128)(2,1)}), bf16[8,32,2304]{2,1,0:T(8,128)(2,1)}) %reduce-scatter.13.cloned.1.call-update) | async-done | bytes 1179664 | tf_op jit(solution)/shard_map/reduce_scatter | solution.py:53
  154.8 49.3 %all-gather.15.cloned.1.call-done = bf16[8,256,2304]{2,1,0:T(8,128)(2,1)} async-done(((bf16[8,32,2304]{2,1,0:T(8,128)(2,1)}), bf16[8,256,2304]{2,1,0:T(8,128)(2,1)}) %all-gather.15.cloned.1.call-update) | async-done | bytes 9437200 | tf_op jit(solution)/shard_map/all_gather | solution.py:56
  224.2 18.6 convolution_convert_fusion.5
  243.0 52.9 %reduce-scatter.15.cloned.1.call-done = bf16[8,32,2304]{2,1,0:T(8,128)(2,1)} async-done(((bf16[8,256,2304]{2,1,0:T(8,128)(2,1)}), bf16[8,32,2304]{2,1,0:T(8,128)(2,1)}) %reduce-scatter.15.cloned.1.call-update) | async-done | bytes 1179664 | tf_op jit(solution)/shard_map/reduce_scatter | solution.py:60
  300.8 50.3 %all-gather.17.cloned.1.call-done = bf16[8,256,2304]{2,1,0:T(8,128)(2,1)} async-done(((bf16[8,32,2304]{2,1,0:T(8,128)(2,1)}), bf16[8,256,2304]{2,1,0:T(8,128)(2,1)}) %all-gather.17.cloned.1.call-update) | async-done | bytes 9437200 | tf_op jit(solution)/shard_map/all_gather | solution.py:49
  379.7 52.9 %reduce-scatter.17.cloned.1.call-done = bf16[8,32,2304]{2,1,0:T(8,128)(2,1)} async-done(((bf16[8,256,2304]{2,1,0:T(8,128)(2,1)}), bf16[8,32,2304]{2,1,0:T(8,128)(2,1)}) %reduce-scatter.17.cloned.1.call-update) | async-done | bytes 1179664 | tf_op jit(solution)/shard_map/reduce_scatter | solution.py:53
  437.5 50.3 %all-gather.19.cloned.1.call-done = bf16[8,256,2304]{2,1,0:T(8,128)(2,1)} async-done(((bf16[8,32,2304]{2,1,0:T(8,128)(2,1)}), bf16[8,256,2304]{2,1,0:T(8,128)(2,1)}) %all-gather.19.cloned.1.call-update) | async-done | bytes 9437200 | tf_op jit(solution)/shard_map/all_gather | solution.py:56
  507.8 18.6 convolution_convert_fusion.4
  526.6 52.9 %reduce-scatter.19.cloned.1.call-done = bf16[8,32,2304]{2,1,0:T(8,128)(2,1)} async-done(((bf16[8,256,2304]{2,1,0:T(8,128)(2,1)}), bf16[8,32,2304]{2,1,0:T(8,128)(2,1)}) %reduce-scatter.19.cloned.1.call-update) | async-done | bytes 1179664 | tf_op jit(solution)/shard_map/reduce_scatter | solution.py:60
  585.0 50.2 %all-gather.21.cloned.1.call-done = bf16[8,256,2304]{2,1,0:T(8,128)(2,1)} async-done(((bf16[8,32,2304]{2,1,0:T(8,128)(2,1)}), bf16[8,256,2304]{2,1,0:T(8,128)(2,1)}) %all-gather.21.cloned.1.call-update) | async-done | bytes 9437200 | tf_op jit(solution)/shard_map/all_gather | solution.py:49
  663.8 52.9 %reduce-scatter.21.cloned.1.call-done = bf16[8,32,2304]{2,1,0:T(8,128)(2,1)} async-done(((bf16[8,256,2304]{2,1,0:T(8,128)(2,1)}), bf16[8,32,2304]{2,1,0:T(8,128)(2,1)}) %reduce-scatter.21.cloned.1.call-update) | async-done | bytes 1179664 | tf_op jit(solution)/shard_map/reduce_scatter | solution.py:53
  722.7 49.4 %all-gather.23.cloned.1.call-done = bf16[8,256,2304]{2,1,0:T(8,128)(2,1)} async-done(((bf16[8,32,2304]{2,1,0:T(8,128)(2,1)}), bf16[8,256,2304]{2,1,0:T(8,128)(2,1)}) %all-gather.23.cloned.1.call-update) | async-done | bytes 9437200 | tf_op jit(solution)/shard_map/all_gather | solution.py:56
  772.0 18.6 fusion.87
  790.7 33.0 %all-gather.25.cloned.1.call-done = bf16[8,256,2304]{2,1,0:T(8,128)(2,1)} async-done(((bf16[8,32,2304]{2,1,0:T(8,128)(2,1)}), bf16[8,256,2304]{2,1,0:T(8,128)(2,1)}) %all-gather.25.cloned.1.call-update) | async-done | bytes 9437200 | tf_op jit(solution)/shard_map/all_gather | solution.py:68
  823.6 23.1 %fusion.355 = (f32[1152]{0:T(1024)}, bf16[8,256,1152]{2,1,0:T(8,128)(2,1)S(1)}) fusion(f32[8,256,1152]{2,1,0:T(8,128)} %fusion.87, f32[1152]{0:T(1024)S(1)} %copy-done.114, bf16[8,256,2304]{2,1,0:T(8,128)(2,1)} %all-gather.25.cloned.1.call-done, bf16[3,1152,2304]{2,1,0:T(8,128)(2,1)} %param.16), kind=kOutput, calls=%fused_computation.458 | convolution fusion | flops 10928258048 | bytes 28910592 | tf_op jit(solution)/shard_map/bsd,fd->bsf/dot_general | solution.py:69
  866.1 20.6 %convolution_convert_fusion.3 = bf16[8,256,2304]{2,1,0:T(8,128)(2,1)} fusion(bf16[3,1152,2304]{2,1,0:T(8,128)(2,1)} %param.16, f32[8,256,1152]{2,1,0:T(8,128)} %fusion.87, f32[1152]{0:T(1024)S(1)} %copy-done.114), kind=kOutput, calls=%fused_computation.102 | convolution fusion | flops 10899947520 | bytes 24187392 | tf_op jit(solution)/shard_map/bsf,fd->bsd/dot_general | solution.py:59
  886.8 32.2 %reduce-scatter.25.cloned.1.call-done = bf16[8,32,2304]{2,1,0:T(8,128)(2,1)} async-done(((bf16[8,256,2304]{2,1,0:T(8,128)(2,1)}), bf16[8,32,2304]{2,1,0:T(8,128)(2,1)}) %reduce-scatter.25.cloned.1.call-update) | async-done | bytes 1179664 | tf_op jit(solution)/shard_map/reduce_scatter | solution.py:76
  925.8 49.0 %reduce-scatter.23.cloned.1.call-done = bf16[8,32,2304]{2,1,0:T(8,128)(2,1)} async-done(((bf16[8,256,2304]{2,1,0:T(8,128)(2,1)}), bf16[8,32,2304]{2,1,0:T(8,128)(2,1)}) %reduce-scatter.23.cloned.1.call-update) | async-done | bytes 1179664 | tf_op jit(solution)/shard_map/reduce_scatter | solution.py:60
  983.0 50.3 %all-gather.27.cloned.1.call-done = bf16[8,256,2304]{2,1,0:T(8,128)(2,1)} async-done(((bf16[8,32,2304]{2,1,0:T(8,128)(2,1)}), bf16[8,256,2304]{2,1,0:T(8,128)(2,1)}) %all-gather.27.cloned.1.call-update) | async-done | bytes 9437200 | tf_op jit(solution)/shard_map/all_gather | solution.py:79
  1083.7 52.9 %reduce-scatter.27.cloned.1.call-done = bf16[8,32,2304]{2,1,0:T(8,128)(2,1)} async-done(((bf16[8,256,2304]{2,1,0:T(8,128)(2,1)}), bf16[8,32,2304]{2,1,0:T(8,128)(2,1)}) %reduce-scatter.27.cloned.1.call-update) | async-done | bytes 1179664 | tf_op jit(solution)/shard_map/reduce_scatter | solution.py:85
  1145.0 50.5 %all-gather.29.cloned.1.call-done = bf16[8,256,2304]{2,1,0:T(8,128)(2,1)} async-done(((bf16[8,32,2304]{2,1,0:T(8,128)(2,1)}), bf16[8,256,2304]{2,1,0:T(8,128)(2,1)}) %all-gather.29.cloned.1.call-update) | async-done | bytes 9437200 | tf_op jit(solution)/shard_map/all_gather | solution.py:68
  1195.5 23.2 %fusion.356 = (f32[1152]{0:T(1024)}, bf16[8,256,1152]{2,1,0:T(8,128)(2,1)S(1)}) fusion(f32[8,256,1152]{2,1,0:T(8,128)} %copy-done.131, f32[1152]{0:T(1024)S(1)} %copy-done.112, bf16[8,256,2304]{2,1,0:T(8,128)(2,1)} %all-gather.29.cloned.1.call-done, bf16[3,1152,2304]{2,1,0:T(8,128)(2,1)} %param.16), kind=kOutput, calls=%fused_computation.459 | convolution fusion | flops 10928258048 | bytes 28910592 | tf_op jit(solution)/shard_map/bsd,fd->bsf/dot_general | solution.py:69
  1238.0 52.9 %reduce-scatter.29.cloned.1.call-done = bf16[8,32,2304]{2,1,0:T(8,128)(2,1)} async-done(((bf16[8,256,2304]{2,1,0:T(8,128)(2,1)}), bf16[8,32,2304]{2,1,0:T(8,128)(2,1)}) %reduce-scatter.29.cloned.1.call-update) | async-done | bytes 1179664 | tf_op jit(solution)/shard_map/reduce_scatter | solution.py:76
  1299.6 50.3 %all-gather.31.cloned.1.call-done = bf16[8,256,2304]{2,1,0:T(8,128)(2,1)} async-done(((bf16[8,32,2304]{2,1,0:T(8,128)(2,1)}), bf16[8,256,2304]{2,1,0:T(8,128)(2,1)}) %all-gather.31.cloned.1.call-update) | async-done | bytes 9437200 | tf_op jit(solution)/shard_map/all_gather | solution.py:79
  1400.1 52.9 %reduce-scatter.31.cloned.1.call-done = bf16[8,32,2304]{2,1,0:T(8,128)(2,1)} async-done(((bf16[8,256,2304]{2,1,0:T(8,128)(2,1)}), bf16[8,32,2304]{2,1,0:T(8,128)(2,1)}) %reduce-scatter.31.cloned.1.call-update) | async-done | bytes 1179664 | tf_op jit(solution)/shard_map/reduce_scatter | solution.py:85
  1461.5 50.5 %all-gather.33.cloned.1.call-done = bf16[8,256,2304]{2,1,0:T(8,128)(2,1)} async-done(((bf16[8,32,2304]{2,1,0:T(8,128)(2,1)}), bf16[8,256,2304]{2,1,0:T(8,128)(2,1)}) %all-gather.33.cloned.1.call-update) | async-done | bytes 9437200 | tf_op jit(solution)/shard_map/all_gather | solution.py:68
  1511.9 23.2 %fusion.357 = (f32[1152]{0:T(1024)}, bf16[8,256,1152]{2,1,0:T(8,128)(2,1)S(1)}) fusion(f32[8,256,1152]{2,1,0:T(8,128)} %copy-done.130, f32[1152]{0:T(1024)S(1)} %copy-done.109, bf16[8,256,2304]{2,1,0:T(8,128)(2,1)} %all-gather.33.cloned.1.call-done, bf16[3,1152,2304]{2,1,0:T(8,128)(2,1)} %param.16), kind=kOutput, calls=%fused_computation.460 | convolution fusion | flops 10928258048 | bytes 28910592 | tf_op jit(solution)/shard_map/bsd,fd->bsf/dot_general | solution.py:69
  1555.6 17.8 fusion.12
  1619.0 19.0 %fusion.16 = bf16[1,1152,2304]{2,1,0:T(8,128)(2,1)} fusion(bf16[8,256,2304]{2,1,0:T(8,128)(2,1)} %all-gather.29.cloned.1.call-done, f32[8,256,1152]{2,1,0:T(8,128)} %copy-done.131, f32[1152]{0:T(1024)S(1)} %copy-done.113), kind=kOutput, calls=%fused_computation.43 | convolution fusion | flops 10897883136 | bytes 24187392 | tf_op jit(solution)/shard_map/bsf,bsd->fd/dot_general | solution.py:70
  1672.7 17.6 fusion.14
  1817.4 45.8 %all-reduce.2.cloned.1.call-done = f32[3,6,2304]{2,1,0:T(8,128)} async-done(((f32[3,6,2304]{2,1,0:T(8,128)}), f32[3,6,2304]{2,1,0:T(8,128)}) %all-reduce.2.cloned.1.call-update) | async-done | bytes 165904 | tf_op jit(solution)/shard_map/psum | solution.py:106
  (542 shorter events, 568.1 us)
Async XLA Ops:
  7.2 59.3 %all-gather.13.cloned.1.call-start = ((), (), s32[]{:S(2)}) async-start(), calls=%async_computation.12 | async-start | bytes 10616832 | tf_op jit(solution)/shard_map/all_gather | solution.py:49
  11.0 140.4 %copy-start.42 = (f32[2304]{0:T(1024)}, f32[2304]{0:T(1024)S(1)}, u32[]{:S(2)}) copy-start(f32[2304]{0:T(1024)S(1)} %get-tuple-element.45) | copy-start | bytes 27652
  11.0 287.0 %copy-start.44 = (f32[2304]{0:T(1024)}, f32[2304]{0:T(1024)S(1)}, u32[]{:S(2)}) copy-start(f32[2304]{0:T(1024)S(1)} %get-tuple-element.42) | copy-start | bytes 27652
  11.0 423.6 %copy-start.46 = (f32[2304]{0:T(1024)}, f32[2304]{0:T(1024)S(1)}, u32[]{:S(2)}) copy-start(f32[2304]{0:T(1024)S(1)} %get-tuple-element.39) | copy-start | bytes 27652
  13.2 134.8 %reduce-scatter.13.cloned.1.call-start = ((), (), s32[]{:S(2)}) async-start(), calls=%async_computation.13 | async-start | bytes 10616832 | tf_op jit(solution)/shard_map/reduce_scatter | solution.py:53
  95.0 109.1 %all-gather.15.cloned.1.call-start = ((), (), s32[]{:S(2)}) async-start(), calls=%async_computation.14 | async-start | bytes 10616832 | tf_op jit(solution)/shard_map/all_gather | solution.py:56
  150.4 145.5 %copy-start = (f32[8,32,2304]{2,1,0:T(8,128)}, f32[8,32,2304]{2,1,0:T(8,128)S(1)}, u32[]{:S(2)}) copy-start(f32[8,32,2304]{2,1,0:T(8,128)S(1)} %get-tuple-element.72) | copy-start | bytes 7077892
  153.5 142.4 %reduce-scatter.15.cloned.1.call-start = ((), (), s32[]{:S(2)}) async-start(), calls=%async_computation.15 | async-start | bytes 10616832 | tf_op jit(solution)/shard_map/reduce_scatter | solution.py:60
  154.8 349.5 %copy-start.111 = (f32[1152]{0:T(1024)}, f32[1152]{0:T(1024)S(1)}, u32[]{:S(2)}) copy-start(f32[1152]{0:T(1024)S(1)} %get-tuple-element.52) | copy-start | bytes 13828
  242.9 108.2 %all-gather.17.cloned.1.call-start = ((), (), s32[]{:S(2)}) async-start(), calls=%async_computation.16 | async-start | bytes 10616832 | tf_op jit(solution)/shard_map/all_gather | solution.py:49
  300.6 132.0 %reduce-scatter.17.cloned.1.call-start = ((), (), s32[]{:S(2)}) async-start(), calls=%async_computation.17 | async-start | bytes 10616832 | tf_op jit(solution)/shard_map/reduce_scatter | solution.py:53
  379.6 108.2 %all-gather.19.cloned.1.call-start = ((), (), s32[]{:S(2)}) async-start(), calls=%async_computation.18 | async-start | bytes 10616832 | tf_op jit(solution)/shard_map/all_gather | solution.py:56
  437.2 142.3 %reduce-scatter.19.cloned.1.call-start = ((), (), s32[]{:S(2)}) async-start(), calls=%async_computation.19 | async-start | bytes 10616832 | tf_op jit(solution)/shard_map/reduce_scatter | solution.py:60
  526.5 108.7 %all-gather.21.cloned.1.call-start = ((), (), s32[]{:S(2)}) async-start(), calls=%async_computation.20 | async-start | bytes 10616832 | tf_op jit(solution)/shard_map/all_gather | solution.py:49
  584.7 132.1 %reduce-scatter.21.cloned.1.call-start = ((), (), s32[]{:S(2)}) async-start(), calls=%async_computation.21 | async-start | bytes 10616832 | tf_op jit(solution)/shard_map/reduce_scatter | solution.py:53
  663.8 108.2 %all-gather.23.cloned.1.call-start = ((), (), s32[]{:S(2)}) async-start(), calls=%async_computation.22 | async-start | bytes 10616832 | tf_op jit(solution)/shard_map/all_gather | solution.py:56
  718.8 71.8 %copy-start.103 = (f32[8,32]{1,0:T(8,128)}, f32[8,32]{1,0:T(8,128)S(1)}, u32[]{:S(2)}) copy-start(f32[8,32]{1,0:T(8,128)S(1)} %multiply_reduce_fusion) | copy-start | bytes 3076
  721.5 102.2 %all-gather.25.cloned.1.call-start = ((), (), s32[]{:S(2)}) async-start(), calls=%async_computation.24 | async-start | bytes 10616832 | tf_op jit(solution)/shard_map/all_gather | solution.py:68
  722.1 101.5 %copy-start.114 = (f32[1152]{0:T(1024)S(1)}, f32[1152]{0:T(1024)}, u32[]{:S(2)}) copy-start(f32[1152]{0:T(1024)} %get-tuple-element.50) | copy-start | bytes 13828
  722.1 196.9 %reduce-scatter.25.cloned.1.call-start = ((), (), s32[]{:S(2)}) async-start(), calls=%async_computation.25 | async-start | bytes 10616832 | tf_op jit(solution)/shard_map/reduce_scatter | solution.py:76
  866.0 108.8 %reduce-scatter.23.cloned.1.call-start = ((), (), s32[]{:S(2)}) async-start(), calls=%async_computation.23 | async-start | bytes 10616832 | tf_op jit(solution)/shard_map/reduce_scatter | solution.py:60
  886.7 146.6 %all-gather.27.cloned.1.call-start = ((), (), s32[]{:S(2)}) async-start(), calls=%async_computation.26 | async-start | bytes 10616832 | tf_op jit(solution)/shard_map/all_gather | solution.py:79
  982.7 153.8 %reduce-scatter.27.cloned.1.call-start = ((), (), s32[]{:S(2)}) async-start(), calls=%async_computation.27 | async-start | bytes 10616832 | tf_op jit(solution)/shard_map/reduce_scatter | solution.py:85
  1083.6 111.9 %all-gather.29.cloned.1.call-start = ((), (), s32[]{:S(2)}) async-start(), calls=%async_computation.28 | async-start | bytes 10616832 | tf_op jit(solution)/shard_map/all_gather | solution.py:68
  1144.9 146.0 %reduce-scatter.29.cloned.1.call-start = ((), (), s32[]{:S(2)}) async-start(), calls=%async_computation.29 | async-start | bytes 10616832 | tf_op jit(solution)/shard_map/reduce_scatter | solution.py:76
  1237.9 111.9 %all-gather.31.cloned.1.call-start = ((), (), s32[]{:S(2)}) async-start(), calls=%async_computation.30 | async-start | bytes 10616832 | tf_op jit(solution)/shard_map/all_gather | solution.py:79
  1299.3 153.8 %reduce-scatter.31.cloned.1.call-start = ((), (), s32[]{:S(2)}) async-start(), calls=%async_computation.31 | async-start | bytes 10616832 | tf_op jit(solution)/shard_map/reduce_scatter | solution.py:85
  1400.1 111.9 %all-gather.33.cloned.1.call-start = ((), (), s32[]{:S(2)}) async-start(), calls=%async_computation.32 | async-start | bytes 10616832 | tf_op jit(solution)/shard_map/all_gather | solution.py:68
  1461.4 149.1 %reduce-scatter.33.cloned.1.call-start = ((), (), s32[]{:S(2)}) async-start(), calls=%async_computation.33 | async-start | bytes 10616832 | tf_op jit(solution)/shard_map/reduce_scatter | solution.py:76
  1554.4 136.0 %all-gather.35.cloned.1.call-start = ((), (), s32[]{:S(2)}) async-start(), calls=%async_computation.34 | async-start | bytes 10616832 | tf_op jit(solution)/shard_map/all_gather | solution.py:79
  1618.9 185.1 %reduce-scatter.35.cloned.1.call-start = ((), (), s32[]{:S(2)}) async-start(), calls=%async_computation.35 | async-start | bytes 10616832 | tf_op jit(solution)/shard_map/reduce_scatter | solution.py:85
  1737.7 125.5 %all-reduce.2.cloned.1.call-start = ((), (), s32[]{:S(2)}) async-start(), calls=%async_computation.36 | async-start | bytes 442368 | tf_op jit(solution)/shard_map/psum | solution.py:106
  (160 other events, 2855.0 us)
Sparse Core Ops, SparseCore 0:
  13.3 53.1 all-gather.12
  95.1 52.8 reduce-scatter.12
  153.6 50.3 all-gather.14
  243.0 52.8 reduce-scatter.14
  300.7 50.3 all-gather.16
  379.7 52.8 reduce-scatter.16
  437.4 50.3 all-gather.18
  526.7 52.8 reduce-scatter.18
  584.8 50.3 all-gather.20
  663.9 52.8 reduce-scatter.20
  721.6 50.3 all-gather.22
  773.4 50.1 all-gather.24
  866.1 52.8 reduce-scatter.24
  921.7 53.0 reduce-scatter.22
  982.9 50.3 all-gather.26
  1083.7 52.8 reduce-scatter.26
  1145.1 50.3 all-gather.28
  1238.1 52.8 reduce-scatter.28
  1299.4 50.3 all-gather.30
  1400.2 52.8 reduce-scatter.30
  1461.5 50.3 all-gather.32
  1554.5 52.8 reduce-scatter.32
  1619.0 50.1 all-gather.34
  1737.7 52.8 reduce-scatter.34
  1813.6 49.5 all-reduce.1
where the time goes:
time: 1880 us; the launch traced here: 1870 us
  waiting for transfers between devices  1090 us (58%)
  matrix products  600 us (32%)
  other arithmetic  112 us (6%)
  local copies, waits for them, and re-layouts  51 us (3%)
    reduce_scatter x3, waiting for transfers between devices, layer_fwd(): lax.psum_scatter(attn_part, TENSOR_AXIS, scatter_dimension=1, tiled=True)  159 us
    reduce_scatter x3, waiting for transfers between devices, layer_fwd(): lax.psum_scatter(mlp_part, TENSOR_AXIS, scatter_dimension=1, tiled=True)  155 us
    all_gather x3, waiting for transfers between devices, layer_fwd(): a_full = lax.all_gather(a_shard, TENSOR_AXIS, axis=1, tiled=True)  153 us
    all_gather x3, waiting for transfers between devices, layer_fwd(): m_full = lax.all_gather(m_shard, TENSOR_AXIS, axis=1, tiled=True)  149 us
    all_gather x3, waiting for transfers between devices, layer_bwd(): lax.all_gather(d_cur.astype(jnp.bfloat16), TENSOR_AXIS, axis=1, tiled=True)  134 us
    reduce_scatter x3, waiting for transfers between devices, layer_bwd(): lax.psum_scatter(d_in_part, TENSOR_AXIS, scatter_dimension=1, tiled=True)  106 us
    all_gather x3, waiting for transfers between devices, layer_bwd(): lax.all_gather(d_hid.astype(jnp.bfloat16), TENSOR_AXIS, axis=1, tiled=True)  101 us
    reduce_scatter x3, waiting for transfers between devices, layer_bwd(): lax.psum_scatter(d_mid_part, TENSOR_AXIS, scatter_dimension=1, tiled=True)  85.1 us
  transfers between devices with their start and end apart: 25, of which 22 were waited for; matrix products, arithmetic and copies ran while one was open for 13% of the time, Pallas kernels for 0%

commit v1 on v0

v1 whole, which is shorter than its diff:
```python
import functools
import jax
import jax.numpy as jnp
from jax import lax
from jax.experimental import pallas as pl
from jax.experimental.pallas import tpu as pltpu
from jax.sharding import PartitionSpec as P

TENSOR_AXIS = 'tp'
PARTS_AXIS = 'dp'
MESH = pl.DeviceIdType.MESH
F32 = jnp.float32
BF16 = jnp.bfloat16
GROUPS = 2
LANES = 128
N_COPIES = 23
VMEM_LIMIT = 67043328
ANY = pl.BlockSpec(memory_space=pl.ANY)
VMEM = pl.BlockSpec(memory_space=pltpu.VMEM)
SMEM = pl.BlockSpec(memory_space=pltpu.SMEM)


def dot_nn(lhs, rhs):
    return lax.dot_general(lhs, rhs, (((1,), (0,)), ((), ())), preferred_element_type=F32)


def dot_nt(lhs, rhs):
    return lax.dot_general(lhs, rhs, (((1,), (1,)), ((), ())), preferred_element_type=F32)


def dot_tn(lhs, rhs):
    return lax.dot_general(lhs, rhs, (((0,), (0,)), ((), ())), preferred_element_type=F32)


class Ring:
    def __init__(self, n_dev, src, full, pbuf, precv, r_far, r_near, out, send_sem, recv_sem, own_sem):
        self.src, self.full, self.pbuf, self.precv = src, full, pbuf, precv
        self.r_far, self.r_near, self.out = r_far, r_near, out
        self.send_sem, self.recv_sem, self.own_sem = send_sem, recv_sem, own_sem
        self.rows = src.shape[1]
        self.half = self.rows // 2
        n_chips = n_dev // 2
        me = lax.axis_index(TENSOR_AXIS)
        chip, core = me // 2, me % 2
        self.me, self.core = me, core
        self.right_chip, self.left_chip = (chip + 1) % n_chips, (chip + n_chips - 1) % n_chips
        self.far_chip = (chip + 2) % n_chips
        self.chips = (self.far_chip, self.right_chip, self.left_chip, chip)
        self.partner = chip * 2 + 1 - core
        self.right, self.left, self.far = self.right_chip * 2 + core, self.left_chip * 2 + core, self.far_chip * 2 + core
        self.sent = []

    def barrier(self):
        sem = pltpu.get_barrier_semaphore()
        for dev in (self.partner, self.left, self.right):
            pl.semaphore_signal(sem, inc=1, device_id={TENSOR_AXIS: dev}, device_id_type=MESH)
        pl.semaphore_wait(sem, 3)

    def copy(self, grp, idx, src, dst, dev):
        return pltpu.make_async_remote_copy(src_ref=src, dst_ref=dst, send_sem=self.send_sem.at[grp, idx],
                                            recv_sem=self.recv_sem.at[grp, idx], device_id={TENSOR_AXIS: dev}, device_id_type=MESH)

    def start(self, grp, idx, src, dst, dev):
        desc = self.copy(grp, idx, src, dst, dev)
        desc.start()
        self.sent.append(desc)

    def arrive(self, grp, idx, dst, dev):
        self.copy(grp, idx, dst, dst, dev).wait_recv()

    def slot(self, grp, shard, part=None):
        if part is None:
            return self.full.at[grp, pl.ds(pl.multiple_of(shard * self.rows, self.rows), self.rows), :]
        return self.full.at[grp, pl.ds(pl.multiple_of(shard * self.rows + part * self.half, self.half), self.half), :]

    def src_half(self, grp, part):
        return self.src.at[grp, pl.ds(part * self.half, self.half), :]

    def issue_own(self, grp):
        pltpu.make_async_copy(self.src.at[grp], self.slot(grp, self.me), self.own_sem.at[grp]).start()
        self.start(grp, 1, self.src_half(grp, 0), self.slot(grp, self.me, 0), self.right)
        self.start(grp, 3, self.src_half(grp, 1), self.slot(grp, self.me, 1), self.left)
        self.start(grp, 2, self.src_half(grp, 1), self.slot(grp, self.me, 1), self.right)
        self.start(grp, 4, self.src_half(grp, 0), self.slot(grp, self.me, 0), self.left)
        self.start(grp, 0, self.src.at[grp], self.slot(grp, self.me), self.partner)

    def pass_on(self, grp, idx, idx_next, idx_side, shard, part, dev_from, dev_to):
        here = self.slot(grp, shard, part)
        self.arrive(grp, idx, here, dev_from)
        if idx_next is not None:
            self.start(grp, idx_next, here, here, dev_to)
        self.start(grp, idx_side, here, here, self.partner)

    def serve_first(self, grp):
        self.pass_on(grp, 1, 5, 7, self.left, 0, self.left, self.right)
        self.pass_on(grp, 3, 6, 9, self.right, 1, self.right, self.left)

    def serve_second(self, grp):
        self.pass_on(grp, 2, None, 8, self.left, 1, self.left, None)
        self.pass_on(grp, 4, None, 10, self.right, 0, self.right, None)

    def serve_far(self, grp):
        self.pass_on(grp, 5, None, 11, self.far, 0, self.left, None)
        self.pass_on(grp, 6, None, 12, self.far, 1, self.right, None)

    def wait_full(self, grp):
        pltpu.make_async_copy(self.src.at[grp], self.slot(grp, self.me), self.own_sem.at[grp]).wait()
        other = 1 - self.core
        left, right, far = self.left_chip * 2 + other, self.right_chip * 2 + other, self.far_chip * 2 + other
        self.arrive(grp, 0, self.slot(grp, self.partner), self.partner)
        for idx, shard, part in ((7, left, 0), (9, right, 1), (8, left, 1), (10, right, 0), (11, far, 0), (12, far, 1)):
            self.arrive(grp, idx, self.slot(grp, shard, part), self.partner)

    def send_part(self, grp, k):
        self.start(grp, 13 + k, self.pbuf.at[grp, k, 1 - self.core], self.precv.at[grp, k], self.partner)

    def sum_part(self, grp, k):
        mine = self.precv.at[grp, k]
        self.arrive(grp, 13 + k, mine, self.partner)
        total = self.pbuf[grp, k, self.core].astype(F32) + mine[...].astype(F32)
        mine[...] = total.astype(BF16)
        first, second = mine.at[pl.ds(0, self.half), :], mine.at[pl.ds(self.half, self.half), :]
        if k == 0:
            self.start(grp, 17, first, self.r_far.at[grp, 0], self.right)
            self.start(grp, 18, second, self.r_far.at[grp, 1], self.left)
        elif k == 1:
            self.start(grp, 19, second, self.r_near.at[grp, 0, pl.ds(self.half, self.half), :], self.right)
        elif k == 2:
            self.start(grp, 20, first, self.r_near.at[grp, 1, pl.ds(0, self.half), :], self.left)

    def relay(self, grp):
        for k, side, part, idx_in, idx_out, dev_from, dev_to in (
                (1, 0, 0, 17, 21, self.left, self.right), (2, 1, 1, 18, 22, self.right, self.left)):
            landed = self.r_far.at[grp, side]
            self.arrive(grp, idx_in, landed, dev_from)
            part_rows = pl.ds(part * self.half, self.half)
            mine = self.precv.at[grp, k, part_rows, :]
            mine[...] = (mine[...].astype(F32) + landed[...].astype(F32)).astype(BF16)
            self.start(grp, idx_out, mine, self.r_near.at[grp, side, part_rows, :], dev_to)

    def finish(self, grp):
        low, high = pl.ds(0, self.half), pl.ds(self.half, self.half)
        self.arrive(grp, 19, self.r_near.at[grp, 0, high, :], self.left)
        self.arrive(grp, 20, self.r_near.at[grp, 1, low, :], self.right)
        self.arrive(grp, 21, self.r_near.at[grp, 0, low, :], self.left)
        self.arrive(grp, 22, self.r_near.at[grp, 1, high, :], self.right)
        total = self.precv[grp, 3].astype(F32) + self.r_near[grp, 0].astype(F32) + self.r_near[grp, 1].astype(F32)
        self.out[grp] = total.astype(BF16)

    def drain(self):
        for desc in self.sent:
            desc.wait_send()


def run_schedule(ring, stages, part_dot, on_full, head=((), (), ()), tail=((), (), ())):
    def fill(work):
        for fn in work:
            fn()

    def parts(grp, k):
        rows = ring.rows
        row0 = pl.multiple_of(ring.chips[k] * 2 * rows, 2 * rows)
        width = ring.out.shape[2]
        tile = width // 3

        def column(step, carry):
            cols = pl.ds(pl.multiple_of(step * tile, tile), tile)
            val = part_dot(grp, row0, 2 * rows, step * tile, tile).astype(BF16)
            ring.pbuf[grp, k, 0, :, cols] = val[:rows]
            ring.pbuf[grp, k, 1, :, cols] = val[rows:]
            return carry
        lax.fori_loop(0, 3, column, 0)
        ring.send_part(grp, k)

    ring.issue_own(0)
    fill(head[0])
    ring.serve_first(0)
    ring.issue_own(1)
    fill(head[1])
    ring.serve_second(0)
    fill(head[2])
    ring.serve_far(0)
    ring.wait_full(0)
    on_full(0)
    stages_0 = stages(0)
    stages_0[0]()
    ring.serve_first(1)
    for fn in stages_0[1:]:
        fn()
    parts(0, 0)
    ring.serve_second(1)
    parts(0, 1)
    ring.sum_part(0, 0)
    parts(0, 2)
    ring.sum_part(0, 1)
    parts(0, 3)
    ring.sum_part(0, 2)
    ring.serve_far(1)
    ring.sum_part(0, 3)
    ring.wait_full(1)
    on_full(1)
    stages_1 = stages(1)
    stages_1[0]()
    ring.relay(0)
    for fn in stages_1[1:]:
        fn()
    parts(1, 0)
    parts(1, 1)
    ring.sum_part(1, 0)
    parts(1, 2)
    ring.sum_part(1, 1)
    parts(1, 3)
    ring.sum_part(1, 2)
    fill(tail[0])
    ring.finish(0)
    ring.sum_part(1, 3)
    fill(tail[1])
    ring.relay(1)
    fill(tail[2])
    ring.finish(1)
    ring.drain()


def row_blocks(n_rows, block, body):
    def step(i, carry):
        body(pl.multiple_of(i * block, block))
        return carry
    lax.fori_loop(0, n_rows // block, step, 0)


class Stager:
    def __init__(self, buf, sem):
        self.buf, self.sem, self.pending, self.count = buf, sem, [None, None], 0

    def put(self, pieces, view, dst):
        slot = self.count % 2
        self.count += 1
        if self.pending[slot] is not None:
            self.pending[slot].wait()
        start = 0
        for piece in pieces:
            val = piece().astype(self.buf.dtype)
            lanes = pl.ds(start, val.shape[1])
            start += val.shape[1]
            if len(self.buf.shape) == 4:
                self.buf[slot, :, :, lanes] = val.reshape(self.buf.shape[1], self.buf.shape[2], val.shape[1])
            else:
                self.buf[slot, :, lanes] = val
        copy = pltpu.make_async_copy(view(self.buf.at[slot]), dst, self.sem.at[slot])
        copy.start()
        self.pending[slot] = copy

    def drain(self):
        for copy in self.pending:
            if copy is not None:
                copy.wait()


def load_heads(hbm, vmem, sem, pad):
    head_dim = hbm.shape[1]
    copy = pltpu.make_async_copy(hbm, vmem.at[:, pl.ds(0, head_dim), :], sem)
    copy.start()
    if pad:
        vmem[:, head_dim:, :] = jnp.zeros((vmem.shape[0], LANES - head_dim, vmem.shape[2]), vmem.dtype)
    return copy


def softmax_probs(q_val, k_val, length, scale):
    scores = dot_nt(q_val, k_val) * scale
    row = lax.broadcasted_iota(jnp.int32, scores.shape, 0)
    col = lax.broadcasted_iota(jnp.int32, scores.shape, 1)
    scores = jnp.where((col <= row) & (col < length), scores, -1e30)
    expd = jnp.exp(scores - jnp.max(scores, axis=1, keepdims=True))
    return expd / jnp.sum(expd, axis=1, keepdims=True)


def seq_rows(ref, grp, seq, head):
    block = ref[grp, :, seq, :, head * LANES:(head + 1) * LANES]
    return block.reshape(block.shape[0] * block.shape[1], LANES)


def put_seq(ref, grp, seq, head, val):
    n_dev, pos = ref.shape[1], ref.shape[3]
    ref[grp, :, seq, :, head * LANES:(head + 1) * LANES] = val.reshape(n_dev, pos, LANES)


def attn_fwd_kernel(n_dev, n_heads, scale, src, lengths, w_in, w_out, out, full_out, qkv_out, ctx_out,
                    full, qkv, ctx, w_in_v, w_out_v, pbuf, precv, r_far, r_near, send_sem, recv_sem, own_sem, local_sem):
    ring = Ring(n_dev, src, full, pbuf, precv, r_far, r_near, out, send_sem, recv_sem, own_sem)
    ring.barrier()
    load_in = load_heads(w_in, w_in_v, local_sem.at[0], True)
    load_out = load_heads(w_out, w_out_v, local_sem.at[1], True)
    saves = []
    n_seq, pos = qkv.shape[2], qkv.shape[3]
    n_rows, d_model = full.shape[1], full.shape[2]
    shard_rows = n_seq * pos

    def save(src_ref, dst_ref, idx):
        copy = pltpu.make_async_copy(src_ref, dst_ref, local_sem.at[idx])
        copy.start()
        saves.append(copy)

    def on_full(grp):
        if grp == 0:
            load_in.wait()
            load_out.wait()
        save(full.at[grp], full_out.at[grp], 2 + grp)

    def stages(grp):
        def project():
            def body(row0):
                w_all = w_in_v[...].reshape(w_in_v.shape[0] * LANES, d_model)
                val = dot_nt(full[grp, pl.ds(row0, 2 * shard_rows), :], w_all).astype(BF16)
                dev0 = row0 // shard_rows
                qkv[grp, pl.ds(dev0, 2)] = val.reshape(2, n_seq, pos, val.shape[1])
            row_blocks(n_rows, 2 * shard_rows, body)

        def attend():
            def one_seq(seq, carry):
                length = lengths[grp * n_seq + seq]
                for head in range(n_heads):
                    prob = softmax_probs(seq_rows(qkv, grp, seq, head), seq_rows(qkv, grp, seq, n_heads + head), length, scale)
                    val = dot_nn(prob.astype(BF16), seq_rows(qkv, grp, seq, 2 * n_heads + head))
                    put_seq(ctx, grp, seq, head, val.astype(BF16))
                return carry
            lax.fori_loop(0, n_seq, one_seq, 0)
            save(qkv.at[grp], qkv_out.at[grp], 4 + grp)
            save(ctx.at[grp], ctx_out.at[grp], 6 + grp)
        return [project, attend]

    def part_dot(grp, row0, rows, col0, tile):
        lhs = ctx[grp, pl.ds(row0 // shard_rows, rows // shard_rows)].reshape(rows, n_heads * LANES)
        w_cols = w_out_v[:, :, pl.ds(pl.multiple_of(col0, tile), tile)].reshape(n_heads * LANES, tile)
        return dot_nn(lhs, w_cols)

    run_schedule(ring, stages, part_dot, on_full)
    for copy in saves:
        copy.wait()


def attn_bwd_kernel(n_dev, n_heads, scale, src, lengths, w_in, w_out, qkv_hbm, ctx_hbm, a_hbm, m_hbm, dpre_hbm,
                    out, g_in, g_out, g_up, full, act, qkv, dctx, dqkv, w_in_v, w_out_v, stage, stage_sem,
                     pbuf, precv, r_far, r_near, send_sem, recv_sem, own_sem, local_sem):
    ring = Ring(n_dev, src, full, pbuf, precv, r_far, r_near, out, send_sem, recv_sem, own_sem)
    ring.barrier()
    stager = Stager(stage, stage_sem.at[0])
    load_m = pltpu.make_async_copy(m_hbm, act, local_sem.at[2])
    load_dpre = pltpu.make_async_copy(dpre_hbm, dqkv, local_sem.at[3])
    load_dpre.start()
    load_m.start()
    load_out = load_heads(w_out, w_out_v, local_sem.at[1], True)
    load_qkv = pltpu.make_async_copy(qkv_hbm, qkv, local_sem.at[6])
    load_ctx = pltpu.make_async_copy(ctx_hbm, dctx, local_sem.at[4])
    load_qkv.start()
    load_in = load_heads(w_in, w_in_v, local_sem.at[0], True)
    load_a = pltpu.make_async_copy(a_hbm, act, local_sem.at[5])
    n_seq, pos = qkv.shape[2], qkv.shape[3]
    n_rows, d_model = full.shape[1], full.shape[2]
    shard_rows = n_seq * pos
    tile = n_heads * LANES
    head_dim = w_out.shape[1]

    def on_full(grp):
        if grp == 0:
            load_in.wait()
            load_out.wait()
            load_qkv.wait()
            load_a.start()

    def stages(grp):
        def project():
            def body(row0):
                w_all = w_out_v[...].reshape(n_heads * LANES, d_model)
                val = dot_nt(full[grp, pl.ds(row0, 2 * shard_rows), :], w_all).astype(BF16)
                dctx[grp, pl.ds(row0 // shard_rows, 2)] = val.reshape(2, n_seq, pos, val.shape[1])
            row_blocks(n_rows, 2 * shard_rows, body)

        def attend():
            def one_seq(seq, carry):
                length = lengths[grp * n_seq + seq]
                for head in range(n_heads):
                    q_val, k_val = seq_rows(qkv, grp, seq, head), seq_rows(qkv, grp, seq, n_heads + head)
                    v_val, dc_val = seq_rows(qkv, grp, seq, 2 * n_heads + head), seq_rows(dctx, grp, seq, head)
                    prob = softmax_probs(q_val, k_val, length, scale)
                    d_prob = dot_nt(dc_val, v_val).astype(BF16).astype(F32)
                    d_score = prob * (d_prob - jnp.sum(d_prob * prob, axis=1, keepdims=True))
                    d_score = (d_score * scale).astype(BF16)
                    put_seq(dqkv, grp, seq, head, dot_nn(d_score, k_val).astype(BF16))
                    put_seq(dqkv, grp, seq, n_heads + head, dot_tn(d_score, q_val).astype(BF16))
                    put_seq(dqkv, grp, seq, 2 * n_heads + head, dot_tn(prob.astype(BF16), dc_val).astype(BF16))
                return carry
            lax.fori_loop(0, n_seq, one_seq, 0)
            if grp + 1 == GROUPS:
                load_ctx.start()
        return [project, attend]

    def part_dot(grp, row0, rows, col0, width):
        n_cols = dqkv.shape[4]
        lhs = dqkv[grp, pl.ds(row0 // shard_rows, rows // shard_rows)].reshape(rows, n_cols)
        w_cols = w_in_v[:, :, pl.ds(pl.multiple_of(col0, width), width)].reshape(n_cols, width)
        return dot_nn(lhs, w_cols)

    def up_tile(step):
        def run():
            if step == 0:
                load_dpre.wait()
                load_m.wait()
            cols = pl.ds(step * tile, tile)
            n_cols = dqkv.shape[4]
            stager.put([lambda: dot_tn(act[:, :, cols].reshape(GROUPS * n_rows, tile), dqkv[...].reshape(GROUPS * n_rows, n_cols))], lambda ref: ref.at[:, :, pl.ds(0, n_cols)], g_up.at[pl.ds(step * n_heads, n_heads)])
        return run

    half = d_model // 2
    halves = (slice(0, half), slice(half, d_model))

    def heads_view(ref):
        return ref.at[:, pl.ds(0, head_dim), :]

    def out_grad():
        load_ctx.wait()
        stager.put([lambda lanes=lanes: dot_tn(dctx[...].reshape(GROUPS * n_rows, tile), full[:, :, lanes].reshape(GROUPS * n_rows, half))
                    for lanes in halves], heads_view, g_out)

    def in_tile(kind):
        def run():
            if kind == 0:
                load_a.wait()
            cols = pl.ds(kind * tile, tile)
            stager.put([lambda lanes=lanes: dot_tn(dqkv[:, :, :, :, cols].reshape(GROUPS * n_rows, tile), act[:, :, lanes].reshape(GROUPS * n_rows, half))
                        for lanes in halves], heads_view, g_in.at[pl.ds(kind * n_heads, n_heads)])
        return run

    n_up = d_model // tile
    ups = [up_tile(step) for step in range(n_up)]
    head = (ups[:n_up // 3], ups[n_up // 3:2 * (n_up // 3)], ups[2 * (n_up // 3):])
    run_schedule(ring, stages, part_dot, on_full, head, ([out_grad], [in_tile(0)], [in_tile(1), in_tile(2)]))
    stager.drain()


def gelu_tanh(pre_act):
    return jax.nn.gelu(pre_act, approximate=True)


def mlp_fwd_kernel(n_dev, src, w_up, b_up, w_down, out, full_out, pre_out,
                   full, pre, act, w_up_v, w_down_v, pbuf, precv, r_far, r_near, send_sem, recv_sem, own_sem, local_sem):
    ring = Ring(n_dev, src, full, pbuf, precv, r_far, r_near, out, send_sem, recv_sem, own_sem)
    ring.barrier()
    load_in = pltpu.make_async_copy(w_up, w_up_v, local_sem.at[0])
    load_out = pltpu.make_async_copy(w_down, w_down_v, local_sem.at[1])
    load_in.start()
    load_out.start()
    saves = []
    n_rows = full.shape[1]
    block = 2 * ring.rows

    def save(src_ref, dst_ref, idx):
        copy = pltpu.make_async_copy(src_ref, dst_ref, local_sem.at[idx])
        copy.start()
        saves.append(copy)

    def on_full(grp):
        if grp == 0:
            load_in.wait()
            load_out.wait()
        save(full.at[grp], full_out.at[grp], 2 + grp)

    def stages(grp):
        def project():
            def body(row0):
                rows = pl.ds(row0, block)
                val = dot_nn(full[grp, rows, :], w_up_v[...]) + b_up[...]
                pre[grp, rows, :] = val
                act[grp, rows, :] = gelu_tanh(val).astype(BF16)
            row_blocks(n_rows, block, body)
            save(pre.at[grp], pre_out.at[grp], 4 + grp)
        return [project]

    def part_dot(grp, row0, rows, col0, tile):
        return dot_nn(act[grp, pl.ds(row0, rows), :], w_down_v[:, pl.ds(pl.multiple_of(col0, tile), tile)])

    run_schedule(ring, stages, part_dot, on_full)
    for copy in saves:
        copy.wait()


def gelu_tanh_and_grad(pre_act, grad):
    coef = 0.7978845608028654
    square = pre_act * pre_act
    tanh_val = jnp.tanh(coef * (pre_act + 0.044715 * (square * pre_act)))
    cdf = 0.5 * (1.0 + tanh_val)
    slope = coef * (1.0 + 3.0 * 0.044715 * square)
    return pre_act * cdf, grad * (cdf + 0.5 * pre_act * (1.0 - tanh_val * tanh_val) * slope)


def mlp_bwd_kernel(n_dev, src, w_up, w_down, pre_hbm, out, dpre_out, dbias_out, g_down,
                   full, pre, act, dpre, w_up_v, w_down_v, stage, stage_sem,
                   pbuf, precv, r_far, r_near, send_sem, recv_sem, own_sem, local_sem):
    ring = Ring(n_dev, src, full, pbuf, precv, r_far, r_near, out, send_sem, recv_sem, own_sem)
    ring.barrier()
    stager = Stager(stage, stage_sem.at[0])
    load_in = pltpu.make_async_copy(w_up, w_up_v, local_sem.at[0])
    load_out = pltpu.make_async_copy(w_down, w_down_v, local_sem.at[1])
    load_pre = [pltpu.make_async_copy(pre_hbm.at[grp], pre, local_sem.at[2 + grp]) for grp in range(GROUPS)]
    for copy in (load_out, load_pre[0], load_in):
        copy.start()
    dbias_out[...] = jnp.zeros_like(dbias_out)
    saves = []
    n_rows = full.shape[1]
    block = 2 * ring.rows
    tile = act.shape[2] // 3

    def on_full(grp):
        if grp == 0:
            load_in.wait()
            load_out.wait()
        load_pre[grp].wait()

    def stages(grp):
        def project():
            def body(row0):
                rows = pl.ds(row0, block)
                d_act = dot_nt(full[grp, rows, :], w_down_v[...]).astype(BF16).astype(F32)
                act_val, d_pre = gelu_tanh_and_grad(pre[rows, :], d_act)
                act[grp, rows, :] = act_val.astype(BF16)
                dbias_out[...] += jnp.sum(d_pre, axis=0, keepdims=True)
                dpre[grp, rows, :] = d_pre.astype(BF16)
            row_blocks(n_rows, block, body)
            if grp + 1 < GROUPS:
                load_pre[grp + 1].start()
            copy = pltpu.make_async_copy(dpre.at[grp], dpre_out.at[grp], local_sem.at[4 + grp])
            copy.start()
            saves.append(copy)
        return [project]

    def part_dot(grp, row0, rows, col0, width):
        return dot_nt(dpre[grp, pl.ds(row0, rows), :], w_up_v[pl.ds(pl.multiple_of(col0, width), width), :])

    def down_tile(step):
        def run():
            cols = pl.ds(step * tile, tile)
            half = full.shape[2] // 2
            stager.put([lambda lanes=lanes: dot_tn(act[:, :, cols].reshape(GROUPS * n_rows, tile), full[:, :, lanes].reshape(GROUPS * n_rows, half))
                        for lanes in (slice(0, half), slice(half, 2 * half))], lambda ref: ref, g_down.at[cols, :])
        return run

    run_schedule(ring, stages, part_dot, on_full, tail=([down_tile(0)], [down_tile(1)], [down_tile(2)]))
    stager.drain()
    for copy in saves:
        copy.wait()


def ring_scratch(n_dev, rows, d_model):
    return [pltpu.VMEM((GROUPS, 4, 2, rows, d_model), BF16), pltpu.VMEM((GROUPS, 4, rows, d_model), BF16),
            pltpu.VMEM((GROUPS, 2, rows // 2, d_model), BF16), pltpu.VMEM((GROUPS, 2, rows, d_model), BF16),
            pltpu.SemaphoreType.DMA((GROUPS, N_COPIES)), pltpu.SemaphoreType.DMA((GROUPS, N_COPIES)),
            pltpu.SemaphoreType.DMA((GROUPS,)), pltpu.SemaphoreType.DMA((8,))]


def call_kernel(kernel, name, collective_id, out_shape, out_specs, in_specs, scratch, flops, args):
    return pl.pallas_call(
        kernel, out_shape=out_shape, in_specs=in_specs, out_specs=out_specs, scratch_shapes=scratch, name=name,
        cost_estimate=pl.CostEstimate(flops=flops, bytes_accessed=40_000_000, transcendentals=0),
        compiler_params=pltpu.CompilerParams(collective_id=collective_id, has_side_effects=True, vmem_limit_bytes=VMEM_LIMIT))(*args)


def shape(dims, dtype):
    return jax.ShapeDtypeStruct(dims, dtype)


def dims_of(shard, n_dev):
    n_seq, pos, d_model = shard.shape[0] // GROUPS, shard.shape[1], shard.shape[2]
    return n_seq, pos, n_seq * pos, n_dev * n_seq * pos, d_model


def attn_fwd(shard, lengths, w_in, w_out, n_dev, collective_id):
    n_seq, pos, rows, n_rows, d_model = dims_of(shard, n_dev)
    n_heads, head_dim = w_out.shape[0], w_out.shape[1]
    n_cols, c_cols = w_in.shape[0] * LANES, n_heads * LANES
    qkv_dims, ctx_dims = (GROUPS, n_dev, n_seq, pos, n_cols), (GROUPS, n_dev, n_seq, pos, c_cols)
    out, full, qkv, ctx = call_kernel(
        functools.partial(attn_fwd_kernel, n_dev, n_heads, head_dim ** -0.5), 'attn_fwd', collective_id,
        (shape((GROUPS, rows, d_model), BF16), shape((GROUPS, n_rows, d_model), BF16), shape(qkv_dims, BF16), shape(ctx_dims, BF16)),
        (VMEM, ANY, ANY, ANY), (VMEM, SMEM, ANY, ANY),
        [pltpu.VMEM((GROUPS, n_rows, d_model), BF16), pltpu.VMEM(qkv_dims, BF16), pltpu.VMEM(ctx_dims, BF16),
         pltpu.VMEM((w_in.shape[0], LANES, d_model), BF16), pltpu.VMEM((n_heads, LANES, d_model), BF16)] + ring_scratch(n_dev, rows, d_model),
        2 * GROUPS * n_rows * d_model * (n_cols + c_cols), (shard.reshape(GROUPS, rows, d_model), lengths, w_in, w_out))
    return out.reshape(shard.shape), full, qkv, ctx


def attn_bwd(shard, lengths, w_in, w_out, qkv, ctx, a_full, m_full, dpre, n_dev, collective_id):
    n_seq, pos, rows, n_rows, d_model = dims_of(shard, n_dev)
    n_heads, head_dim = w_out.shape[0], w_out.shape[1]
    n_cols, c_cols, ff = w_in.shape[0] * LANES, n_heads * LANES, dpre.shape[2]
    return call_kernel(
        functools.partial(attn_bwd_kernel, n_dev, n_heads, head_dim ** -0.5), 'attn_bwd', collective_id,
        (shape((GROUPS, rows, d_model), BF16), shape(w_in.shape, BF16), shape(w_out.shape, BF16), shape((d_model // LANES, LANES, ff), BF16)),
        (VMEM, ANY, ANY, ANY), (VMEM, SMEM) + (ANY,) * 7,
        [pltpu.VMEM((GROUPS, n_rows, d_model), BF16), pltpu.VMEM((GROUPS, n_rows, d_model), BF16),
         pltpu.VMEM(qkv.shape, BF16), pltpu.VMEM(ctx.shape, BF16), pltpu.VMEM(qkv.shape, BF16),
         pltpu.VMEM((w_in.shape[0], LANES, d_model), BF16), pltpu.VMEM((n_heads, LANES, d_model), BF16),
         pltpu.VMEM((2, n_heads, LANES, d_model), BF16), pltpu.SemaphoreType.DMA((1, 2))] + ring_scratch(n_dev, rows, d_model),
        4 * GROUPS * n_rows * d_model * (n_cols + c_cols), (shard.reshape(GROUPS, rows, d_model), lengths, w_in, w_out, qkv, ctx, a_full, m_full, dpre.reshape(qkv.shape)))


def mlp_fwd(shard, w_up, b_up, w_down, n_dev, collective_id):
    n_seq, pos, rows, n_rows, d_model = dims_of(shard, n_dev)
    ff = w_up.shape[1]
    out, full, pre = call_kernel(
        functools.partial(mlp_fwd_kernel, n_dev), 'mlp_fwd', collective_id,
        (shape((GROUPS, rows, d_model), BF16), shape((GROUPS, n_rows, d_model), BF16), shape((GROUPS, n_rows, ff), F32)),
        (VMEM, ANY, ANY), (VMEM, ANY, VMEM, ANY),
        [pltpu.VMEM((GROUPS, n_rows, d_model), BF16), pltpu.VMEM((GROUPS, n_rows, ff), F32), pltpu.VMEM((GROUPS, n_rows, ff), BF16),
         pltpu.VMEM(w_up.shape, BF16), pltpu.VMEM(w_down.shape, BF16)] + ring_scratch(n_dev, rows, d_model),
        4 * GROUPS * n_rows * d_model * ff, (shard.reshape(GROUPS, rows, d_model), w_up, b_up.reshape(1, ff), w_down))
    return out.reshape(shard.shape), full, pre


def mlp_bwd(shard, w_up, w_down, pre, n_dev, collective_id):
    n_seq, pos, rows, n_rows, d_model = dims_of(shard, n_dev)
    ff = w_up.shape[1]
    return call_kernel(
        functools.partial(mlp_bwd_kernel, n_dev), 'mlp_bwd', collective_id,
        (shape((GROUPS, rows, d_model), BF16), shape((GROUPS, n_rows, ff), BF16), shape((1, ff), F32), shape(w_down.shape, BF16)),
        (VMEM, ANY, VMEM, ANY), (VMEM, ANY, ANY, ANY),
        [pltpu.VMEM((GROUPS, n_rows, d_model), BF16), pltpu.VMEM((n_rows, ff), F32), pltpu.VMEM((GROUPS, n_rows, ff), BF16), pltpu.VMEM((GROUPS, n_rows, ff), BF16),
         pltpu.VMEM(w_up.shape, BF16), pltpu.VMEM(w_down.shape, BF16), pltpu.VMEM((2, ff // 3, d_model), BF16), pltpu.SemaphoreType.DMA((1, 2))] + ring_scratch(n_dev, rows, d_model),
        6 * GROUPS * n_rows * d_model * ff, (shard.reshape(GROUPS, rows, d_model), w_up, w_down, pre))


def sum_kernel(n_dev, parts, out, landed, total, send_sem, recv_sem):
    me = lax.axis_index(TENSOR_AXIS)
    others = [(me + step) % n_dev for step in range(1, n_dev)]
    sem = pltpu.get_barrier_semaphore()
    for dev in others:
        pl.semaphore_signal(sem, inc=1, device_id={TENSOR_AXIS: dev}, device_id_type=MESH)
    pl.semaphore_wait(sem, n_dev - 1)

    def copy(phase, idx, src_ref, dst_ref, dev):
        return pltpu.make_async_remote_copy(src_ref=src_ref, dst_ref=dst_ref, send_sem=send_sem.at[phase, idx], recv_sem=recv_sem.at[phase, idx],
                                            device_id={TENSOR_AXIS: dev}, device_id_type=MESH)
    sent = [copy(0, idx, parts.at[dev], landed.at[idx], dev) for idx, dev in enumerate(others)]
    for desc in sent:
        desc.start()
    acc = parts[me]
    for idx in range(n_dev - 1):
        sent[idx].wait_recv()
        acc = acc + landed[idx]
    total[...] = acc
    out[me] = acc
    spread = [copy(1, idx, total, out.at[me], dev) for idx, dev in enumerate(others)]
    for desc in spread:
        desc.start()
    for idx in range(n_dev - 1):
        origin = (me + n_dev - 1 - idx) % n_dev
        copy(1, idx, total, out.at[origin], origin).wait_recv()
    for desc in sent + spread:
        desc.wait_send()


def sum_over_devices(val, n_dev, collective_id):
    size = val.size
    per_dev = -(-size // (n_dev * LANES)) * LANES
    flat = jnp.pad(val.reshape(-1), (0, per_dev * n_dev - size)).reshape(n_dev, per_dev // LANES, LANES)
    out = pl.pallas_call(
        functools.partial(sum_kernel, n_dev), out_shape=shape(flat.shape, F32), in_specs=[VMEM], out_specs=VMEM, name='sum_devices',
        scratch_shapes=[pltpu.VMEM((n_dev - 1,) + flat.shape[1:], F32), pltpu.VMEM(flat.shape[1:], F32),
                        pltpu.SemaphoreType.DMA((2, n_dev - 1)), pltpu.SemaphoreType.DMA((2, n_dev - 1))],
        compiler_params=pltpu.CompilerParams(collective_id=collective_id, has_side_effects=True))(flat)
    return out.reshape(-1)[:size].reshape(val.shape)


def layer_norm(x_val, gain_vec, shift_vec):
    row_mean = jnp.mean(x_val, axis=-1, keepdims=True)
    centered = x_val - row_mean
    row_var = jnp.mean(centered * centered, axis=-1, keepdims=True)
    return centered * lax.rsqrt(row_var + 1e-5) * gain_vec + shift_vec


def layer_fwd(x_cur, lengths, weights, vec_layer, n_dev, collective_id):
    w_in, w_out, w_up, b_up, w_down = weights
    a_shard = layer_norm(x_cur, vec_layer[0], vec_layer[1]).astype(BF16)
    attn_shard, a_full, qkv, ctx = attn_fwd(a_shard, lengths, w_in, w_out, n_dev, collective_id)
    hidden = x_cur + attn_shard.astype(F32) + vec_layer[4]
    m_shard = layer_norm(hidden, vec_layer[2], vec_layer[3]).astype(BF16)
    mlp_shard, m_full, pre = mlp_fwd(m_shard, w_up, b_up, w_down, n_dev, collective_id + 1)
    x_next = hidden + mlp_shard.astype(F32) + vec_layer[5]
    return x_next, (x_cur, a_full, qkv, ctx, hidden, m_full, pre)


def layer_bwd(d_cur, residues, lengths, weights, vec_layer, n_dev, collective_id):
    w_in, w_out, w_up, _, w_down = weights
    x_prev, a_full, qkv, ctx, hidden, m_full, pre = residues
    n_heads, head_dim, d_model = w_out.shape
    d_mid, d_pre, g_bup, g_down = mlp_bwd(d_cur.astype(BF16), w_up, w_down, pre, n_dev, collective_id)
    d_hid_ln, d_gain2, d_shift2 = jax.vjp(layer_norm, hidden, vec_layer[2], vec_layer[3])[1](d_mid.reshape(d_cur.shape).astype(F32))
    d_hid = d_cur + d_hid_ln
    d_in, g_in, g_out, g_up = attn_bwd(d_hid.astype(BF16), lengths, w_in, w_out, qkv, ctx, a_full, m_full, d_pre, n_dev, collective_id + 1)
    d_x_ln, d_gain1, d_shift1 = jax.vjp(layer_norm, x_prev, vec_layer[0], vec_layer[1])[1](d_in.reshape(d_cur.shape).astype(F32))
    g_vec = jnp.stack([d_gain1, d_shift1, d_gain2, d_shift2, jnp.sum(d_hid, axis=(0, 1)), jnp.sum(d_cur, axis=(0, 1))])
    return d_hid + d_x_ln, (g_in, g_out, g_up.reshape(w_up.shape), g_bup[0], g_down, g_vec)


def group_body(n_dev, x_loc, dy_loc, len_loc, wqkv_loc, wout_loc, wup_loc, bup_loc, wdown_loc, vec_loc):
    n_layers, d_model, n_kinds, n_heads, head_dim = wqkv_loc.shape
    w_in_all = jnp.transpose(wqkv_loc, (0, 2, 3, 4, 1)).reshape(n_layers, n_kinds * n_heads, head_dim, d_model)
    saved_acts = []
    x_cur = x_loc
    weights_of = lambda idx: (w_in_all[idx], wout_loc[idx], wup_loc[idx], bup_loc[idx], wdown_loc[idx])
    for layer_idx in range(n_layers):
        x_cur, residues = layer_fwd(x_cur, len_loc, weights_of(layer_idx), vec_loc[layer_idx], n_dev, 2 * layer_idx)
        saved_acts.append(residues)
    d_cur = dy_loc.astype(F32)
    layer_grads = [None] * n_layers
    for layer_idx in reversed(range(n_layers)):
        d_cur, grad_set = layer_bwd(d_cur, saved_acts[layer_idx], len_loc, weights_of(layer_idx), vec_loc[layer_idx], n_dev,
                                    2 * n_layers + 2 * layer_idx)
        layer_grads[layer_idx] = grad_set
    stacked = [jnp.stack([grad_set[grad_pos] for grad_set in layer_grads]) for grad_pos in range(6)]
    g_vec = sum_over_devices(stacked[5], n_dev, 4 * n_layers)
    g_qkv = jnp.transpose(stacked[0].reshape(n_layers, n_kinds, n_heads, head_dim, d_model), (0, 4, 1, 2, 3))
    return x_cur, d_cur, g_qkv, stacked[1], stacked[2], stacked[3], stacked[4], g_vec


def solution(mesh):
    act_spec = P(PARTS_AXIS, TENSOR_AXIS, None)
    in_specs = (act_spec, act_spec, P(PARTS_AXIS), P(None, None, None, TENSOR_AXIS, None), P(None, TENSOR_AXIS, None, None), P(None, None, TENSOR_AXIS), P(None, TENSOR_AXIS), P(None, TENSOR_AXIS, None), P())
    out_specs = (act_spec, act_spec, P(PARTS_AXIS, None, None, TENSOR_AXIS, None), P(PARTS_AXIS, TENSOR_AXIS, None, None), P(PARTS_AXIS, None, TENSOR_AXIS), P(PARTS_AXIS, TENSOR_AXIS), P(PARTS_AXIS, TENSOR_AXIS, None), P(PARTS_AXIS, None, None))
    return jax.shard_map(functools.partial(group_body, mesh.shape[TENSOR_AXIS]), mesh=mesh, in_specs=in_specs, out_specs=out_specs, check_vma=False)
```

time: 1880 us -> 1210 us (0.64)
  waiting for transfers between devices: 1090 us -> 0 us
  Pallas kernels: 0 us -> 1040 us
  matrix products: 600 us -> 0 us
    pallas_call x0 -> x13, Pallas kernels: none -> 1040 us  [the longest x12 1030 us: call_kernel(): pl.pallas_call(kernel, out_shape=out_shape, in_specs=in_specs, out_specs=...]
    dot_general x54 -> x0, matrix products: 600 us -> none  [the longest x3 69.6 us: layer_bwd(): jnp.einsum('bsd,fd->bsf', d_mlp, w_down, preferred_element_type=jnp.float32)]
    all_gather x12 -> x0, waiting for transfers between devices: 537 us -> none  [the longest x3 153 us: layer_fwd(): a_full = lax.all_gather(a_shard, TENSOR_AXIS, axis=1, tiled=True)]
    reduce_scatter x12 -> x0, waiting for transfers between devices: 504 us -> none  [the longest x3 159 us: layer_fwd(): lax.psum_scatter(attn_part, TENSOR_AXIS, scatter_dimension=1, tiled=True)]
    psum x1 -> x0, waiting for transfers between devices: 45.8 us -> none  [group_body(): g_vec = lax.psum(stacked[5], TENSOR_AXIS)]
    unnamed x335 -> x212, local copies, waits for them, and re-layouts: 40.9 us -> 10.3 us
    squeeze x0 -> x3, local copies, waits for them, and re-layouts: none -> 23.5 us  [the longest x1 12.9 us: group_body(): wup_loc[idx]]
  transfers between devices with their start and end apart: 25 -> 0, of which waited for: 22 -> 0; matrix products, arithmetic and copies ran while one was open for 13% -> 0% of each run, Pallas kernels for 0% -> 0%
where the time goes in v1:
time: 1210 us; the launch traced here: 1200 us
  Pallas kernels  1040 us (86%)
  other arithmetic  108 us (9%)
  local copies, waits for them, and re-layouts  50.6 us (4%)
    pallas_call x12, Pallas kernels, call_kernel(): pl.pallas_call(kernel, out_shape=out_shape, in_specs=in_specs, out_specs=...  1030 us
    another operation x5, other arithmetic, group_body(): jnp.stack([grad_set[grad_pos] for grad_set in layer_grads])  28.9 us
    reduce_sum x17, other arithmetic, layer_norm(): return centered * lax.rsqrt(row_var + 1e-05) * gain_vec + shift_vec  27.2 us

profile of v1, /device:TPU:113, one launch (start us, length us, event | category | flops | bytes accessed | tf_op | source)
XLA Modules:
  0.0 1200.4 jit_solution(3266619622445206739)
XLA Ops:
  6.6 4.9 slice_bitcast_fusion.6
  11.6 4.9 fusion.34
  16.4 85.2 %attn_fwd.3 = (bf16[2,128,2304]{2,1,0:T(8,128)(2,1)}, bf16[2,1024,2304]{2,1,0:T(8,128)(2,1)}, bf16[2,8,4,32,1152]{4,3,2,1,0:T(8,128)(2,1)}, bf16[2,8,4,32,384]{4,3,2,1,0:T(8,128)(2,1)}) custom-call(bf16[2,128,2304]{2,1,0:T(8,128)(2,1)} %bitcast.110, s32[8]{0:T(128)} %lengths.11, bf16[9,96,2304]{2,1,0:T(8,128)(2,1)} %bitcast.97, ...), custom_call_target="tpu_custom_call" | custom-call | flops 14495514624 | bytes 40000000 | tf_op jit(solution)/shard_map/attn_fwd/pallas_call | solution.py:560
  101.6 2.4 fusion.32
  106.3 12.9 %slice_bitcast_fusion.1 = (bf16[2304,1152]{1,0:T(8,128)(2,1)}, bf16[2304,1152]{1,0:T(8,128)(2,1)}, bf16[2304,1152]{1,0:T(8,128)(2,1)}) fusion(bf16[3,2304,1152]{2,1,0:T(8,128)(2,1)} %param.14), kind=kLoop, calls=%fused_computation.4 | loop fusion | bytes 31850496 | tf_op jit(solution)/shard_map/squeeze | solution.py:708
  122.1 5.7 slice_bitcast_fusion
  127.8 83.3 %mlp_fwd.3 = (bf16[2,128,2304]{2,1,0:T(8,128)(2,1)}, bf16[2,1024,2304]{2,1,0:T(8,128)(2,1)}, f32[2,1024,1152]{2,1,0:T(8,128)}) custom-call(bf16[2,128,2304]{2,1,0:T(8,128)(2,1)} %bitcast.111, bf16[2304,1152]{1,0:T(8,128)(2,1)} %get-tuple-element.165.w_up, f32[1,1152]{1,0:T(1,128)} %get-tuple-element.177.b_up, bf16[1152,2304]{1,0:T(8,128)(2,1)} %get-tuple-element.162.w_down), custom_call_target="tpu_custom_call" | custom-call | flops 21743271936 | bytes 40000000 | tf_op jit(solution)/shard_map/mlp_fwd/pallas_call | solution.py:560
  211.1 2.4 fusion.30
  215.8 83.0 %attn_fwd.4 = (bf16[2,128,2304]{2,1,0:T(8,128)(2,1)}, bf16[2,1024,2304]{2,1,0:T(8,128)(2,1)}, bf16[2,8,4,32,1152]{4,3,2,1,0:T(8,128)(2,1)}, bf16[2,8,4,32,384]{4,3,2,1,0:T(8,128)(2,1)}) custom-call(bf16[2,128,2304]{2,1,0:T(8,128)(2,1)} %bitcast.116, s32[8]{0:T(128)} %lengths.11, bf16[9,96,2304]{2,1,0:T(8,128)(2,1)} %bitcast.99, ...), custom_call_target="tpu_custom_call" | custom-call | flops 14495514624 | bytes 40000000 | tf_op jit(solution)/shard_map/attn_fwd/pallas_call | solution.py:560
  298.8 2.4 fusion.28
  303.5 83.7 %mlp_fwd.4 = (bf16[2,128,2304]{2,1,0:T(8,128)(2,1)}, bf16[2,1024,2304]{2,1,0:T(8,128)(2,1)}, f32[2,1024,1152]{2,1,0:T(8,128)}) custom-call(bf16[2,128,2304]{2,1,0:T(8,128)(2,1)} %bitcast.117, bf16[2304,1152]{1,0:T(8,128)(2,1)} %get-tuple-element.166.w_up, f32[1,1152]{1,0:T(1,128)} %get-tuple-element.178.b_up, bf16[1152,2304]{1,0:T(8,128)(2,1)} %get-tuple-element.163.w_down), custom_call_target="tpu_custom_call" | custom-call | flops 21743271936 | bytes 40000000 | tf_op jit(solution)/shard_map/mlp_fwd/pallas_call | solution.py:560
  387.3 2.4 fusion.26
  392.0 83.2 %attn_fwd.5 = (bf16[2,128,2304]{2,1,0:T(8,128)(2,1)}, bf16[2,1024,2304]{2,1,0:T(8,128)(2,1)}, bf16[2,8,4,32,1152]{4,3,2,1,0:T(8,128)(2,1)}, bf16[2,8,4,32,384]{4,3,2,1,0:T(8,128)(2,1)}) custom-call(bf16[2,128,2304]{2,1,0:T(8,128)(2,1)} %bitcast.118, s32[8]{0:T(128)} %lengths.11, bf16[9,96,2304]{2,1,0:T(8,128)(2,1)} %bitcast.102, ...), custom_call_target="tpu_custom_call" | custom-call | flops 14495514624 | bytes 40000000 | tf_op jit(solution)/shard_map/attn_fwd/pallas_call | solution.py:560
  475.2 2.4 fusion.24
  479.9 83.7 %mlp_fwd.5 = (bf16[2,128,2304]{2,1,0:T(8,128)(2,1)}, bf16[2,1024,2304]{2,1,0:T(8,128)(2,1)}, f32[2,1024,1152]{2,1,0:T(8,128)}) custom-call(bf16[2,128,2304]{2,1,0:T(8,128)(2,1)} %bitcast.119, bf16[2304,1152]{1,0:T(8,128)(2,1)} %get-tuple-element.164.w_up, f32[1,1152]{1,0:T(1,128)} %get-tuple-element.176.b_up, bf16[1152,2304]{1,0:T(8,128)(2,1)} %get-tuple-element.161.w_down), custom_call_target="tpu_custom_call" | custom-call | flops 21743271936 | bytes 40000000 | tf_op jit(solution)/shard_map/mlp_fwd/pallas_call | solution.py:560
  563.6 84.1 %mlp_bwd.3 = (bf16[2,128,2304]{2,1,0:T(8,128)(2,1)}, bf16[2,1024,1152]{2,1,0:T(8,128)(2,1)}, f32[1,1152]{1,0:T(1,128)}, bf16[1152,2304]{1,0:T(8,128)(2,1)}) custom-call(bf16[2,128,2304]{2,1,0:T(8,128)(2,1)} %bitcast.90, bf16[2304,1152]{1,0:T(8,128)(2,1)} %get-tuple-element.164.w_up, bf16[1152,2304]{1,0:T(8,128)(2,1)} %get-tuple-element.161.w_down, ...), custom_call_target="tpu_custom_call" | custom-call | flops 32614907904 | bytes 40000000 | tf_op jit(solution)/shard_map/mlp_bwd/pallas_call | solution.py:560
  649.8 3.1 multiply_reduce_fusion
  653.6 2.3 fusion.23
  657.7 91.0 %attn_bwd.3 = (bf16[2,128,2304]{2,1,0:T(8,128)(2,1)}, bf16[9,96,2304]{2,1,0:T(8,128)(2,1)}, bf16[3,96,2304]{2,1,0:T(8,128)(2,1)}, bf16[18,128,1152]{2,1,0:T(8,128)(2,1)}) custom-call(bf16[2,128,2304]{2,1,0:T(8,128)(2,1)} %bitcast.120, s32[8]{0:T(128)} %lengths.11, bf16[9,96,2304]{2,1,0:T(8,128)(2,1)} %bitcast.103, ...), custom_call_target="tpu_custom_call" | custom-call | flops 28991029248 | bytes 40000000 | tf_op jit(solution)/shard_map/attn_bwd/pallas_call | solution.py:560
  750.2 2.9 multiply_reduce_fusion.10
  759.5 84.7 %mlp_bwd.4 = (bf16[2,128,2304]{2,1,0:T(8,128)(2,1)}, bf16[2,1024,1152]{2,1,0:T(8,128)(2,1)}, f32[1,1152]{1,0:T(1,128)}, bf16[1152,2304]{1,0:T(8,128)(2,1)}) custom-call(bf16[2,128,2304]{2,1,0:T(8,128)(2,1)} %bitcast.114, bf16[2304,1152]{1,0:T(8,128)(2,1)} %get-tuple-element.166.w_up, bf16[1152,2304]{1,0:T(8,128)(2,1)} %get-tuple-element.163.w_down, ...), custom_call_target="tpu_custom_call" | custom-call | flops 32614907904 | bytes 40000000 | tf_op jit(solution)/shard_map/mlp_bwd/pallas_call | solution.py:560
  846.4 2.8 multiply_reduce_fusion.9
  854.5 90.5 %attn_bwd.4 = (bf16[2,128,2304]{2,1,0:T(8,128)(2,1)}, bf16[9,96,2304]{2,1,0:T(8,128)(2,1)}, bf16[3,96,2304]{2,1,0:T(8,128)(2,1)}, bf16[18,128,1152]{2,1,0:T(8,128)(2,1)}) custom-call(bf16[2,128,2304]{2,1,0:T(8,128)(2,1)} %bitcast.112, s32[8]{0:T(128)} %lengths.11, bf16[9,96,2304]{2,1,0:T(8,128)(2,1)} %bitcast.100, ...), custom_call_target="tpu_custom_call" | custom-call | flops 28991029248 | bytes 40000000 | tf_op jit(solution)/shard_map/attn_bwd/pallas_call | solution.py:560
  946.5 2.9 multiply_reduce_fusion.8
  954.7 84.4 %mlp_bwd.5 = (bf16[2,128,2304]{2,1,0:T(8,128)(2,1)}, bf16[2,1024,1152]{2,1,0:T(8,128)(2,1)}, f32[1,1152]{1,0:T(1,128)}, bf16[1152,2304]{1,0:T(8,128)(2,1)}) custom-call(bf16[2,128,2304]{2,1,0:T(8,128)(2,1)} %bitcast.115, bf16[2304,1152]{1,0:T(8,128)(2,1)} %get-tuple-element.165.w_up, bf16[1152,2304]{1,0:T(8,128)(2,1)} %get-tuple-element.162.w_down, ...), custom_call_target="tpu_custom_call" | custom-call | flops 32614907904 | bytes 40000000 | tf_op jit(solution)/shard_map/mlp_bwd/pallas_call | solution.py:560
  1042.6 2.8 multiply_reduce_fusion.7
  1051.0 90.3 %attn_bwd.5 = (bf16[2,128,2304]{2,1,0:T(8,128)(2,1)}, bf16[9,96,2304]{2,1,0:T(8,128)(2,1)}, bf16[3,96,2304]{2,1,0:T(8,128)(2,1)}, bf16[18,128,1152]{2,1,0:T(8,128)(2,1)}) custom-call(bf16[2,128,2304]{2,1,0:T(8,128)(2,1)} %bitcast.113, s32[8]{0:T(128)} %lengths.11, bf16[9,96,2304]{2,1,0:T(8,128)(2,1)} %bitcast.98, ...), custom_call_target="tpu_custom_call" | custom-call | flops 28991029248 | bytes 40000000 | tf_op jit(solution)/shard_map/attn_bwd/pallas_call | solution.py:560
  1141.3 10.8 maximum_bitcast_fusion
  1152.1 2.5 pad_maximum_fusion.2
  1161.1 12.2 %sum_devices.1 = f32[8,41,128]{2,1,0:T(8,128)} custom-call(f32[8,41,128]{2,1,0:T(8,128)} %reshape.367.parts), custom_call_target="tpu_custom_call" | custom-call | tf_op jit(solution)/shard_map/sum_devices/pallas_call | solution.py:664
  1175.0 13.8 %pad_maximum_fusion = bf16[3,2304,1152]{2,1,0:T(8,128)(2,1)} fusion(bf16[1,2304,1152]{2,1,0:T(8,128)(2,1)} %bitcast.85, bf16[1,2304,1152]{2,1,0:T(8,128)(2,1)} %bitcast.87, bf16[1,2304,1152]{2,1,0:T(8,128)(2,1)} %bitcast.89), kind=kLoop, calls=%fused_computation | loop fusion | flops 15925248 | bytes 31850496 | tf_op jit(solution)/shard_map/stack | solution.py:718
  1188.7 11.3 pad_maximum_fusion.1
  (303 shorter events, 63.6 us)
Async XLA Ops:
  0.7 3.4 copy-start.54
  3.0 3.6 copy-start.44
  3.4 8.1 copy-start.57
  4.0 7.5 copy-start.22
  5.1 6.5 copy-start.30
  106.3 12.9 %slice-start = ((s8[15925248]{0:T(1024)(128)(4,1)}), s8[4194304]{0:T(1024)(128)(4,1)S(1)}, s32[]{:S(2)}) async-start(s8[15925248]{0:T(1024)(128)(4,1)} %bitcast.79), calls=%async_computation | async-start | bytes 8388608
  106.3 13.0 %slice-start.1 = ((s8[15925248]{0:T(1024)(128)(4,1)}), s8[4194304]{0:T(1024)(128)(4,1)S(1)}, s32[]{:S(2)}) async-start(s8[15925248]{0:T(1024)(128)(4,1)} %bitcast.79), calls=%async_computation.1 | async-start | bytes 8388608
  106.3 14.8 %slice-start.2 = ((s8[15925248]{0:T(1024)(128)(4,1)}), s8[4194304]{0:T(1024)(128)(4,1)S(1)}, s32[]{:S(2)}) async-start(s8[15925248]{0:T(1024)(128)(4,1)} %bitcast.79), calls=%async_computation.2 | async-start | bytes 8388608
  106.3 15.8 %slice-start.3 = ((s8[15925248]{0:T(1024)(128)(4,1)}), s8[3342336]{0:T(1024)(128)(4,1)S(1)}, s32[]{:S(2)}) async-start(s8[15925248]{0:T(1024)(128)(4,1)} %bitcast.79), calls=%async_computation.3 | async-start | bytes 6684672
  649.8 3.7 copy-start.88
  649.8 3.7 copy-start.11
  649.8 3.7 copy-start.29
  649.8 3.7 copy-start.43
  649.8 3.8 copy-start.56
  649.8 3.8 copy-start.68
  649.8 3.8 copy-start.69
  750.2 3.0 copy-start.86
  750.2 3.0 copy-start.1
  750.2 3.0 copy-start.33
  750.2 3.0 copy-start.47
  750.2 3.0 copy-start.60
  946.5 3.0 copy-start.7
  946.5 3.0 copy-start.37
  946.5 3.0 copy-start.51
  1141.3 10.8 copy-start.26
  1141.3 10.8 copy-start.27
  1141.3 10.8 copy-start.28
  1152.1 3.4 copy-start.3
  1152.1 3.4 copy-start.31
  1152.1 3.4 copy-start.45
  1157.9 30.9 %slice-start.4 = ((s8[5308416]{0:T(1024)(128)(4,1)}), s8[1114112]{0:T(1024)(128)(4,1)S(1)}, s32[]{:S(2)}) async-start(s8[5308416]{0:T(1024)(128)(4,1)} %bitcast.82), calls=%async_computation.4 | async-start | bytes 2228224
  1175.0 13.8 %slice-start.5 = ((s8[5308416]{0:T(1024)(128)(4,1)}), s8[4194304]{0:T(1024)(128)(4,1)S(1)}, s32[]{:S(2)}) async-start(s8[5308416]{0:T(1024)(128)(4,1)} %bitcast.82), calls=%async_computation.5 | async-start | bytes 8388608
  (74 other events, 140.4 us)

commit v2 on v1

--- a/solution.py
+++ b/solution.py
@@ -48,7 +48,7 @@
         self.chips = (self.far_chip, self.right_chip, self.left_chip, chip)
         self.partner = chip * 2 + 1 - core
         self.right, self.left, self.far = self.right_chip * 2 + core, self.left_chip * 2 + core, self.far_chip * 2 + core
-        self.sent = []
+        self.sent = {}
 
     def barrier(self):
         sem = pltpu.get_barrier_semaphore()
@@ -63,7 +63,7 @@
     def start(self, grp, idx, src, dst, dev):
         desc = self.copy(grp, idx, src, dst, dev)
         desc.start()
-        self.sent.append(desc)
+        self.sent[grp, idx] = desc
 
     def arrive(self, grp, idx, dst, dev):
         self.copy(grp, idx, dst, dst, dev).wait_recv()
@@ -112,12 +112,12 @@
             self.arrive(grp, idx, self.slot(grp, shard, part), self.partner)
 
     def send_part(self, grp, k):
-        self.start(grp, 13 + k, self.pbuf.at[grp, k, 1 - self.core], self.precv.at[grp, k], self.partner)
+        self.start(grp, 13 + k, self.pbuf.at[k, 1 - self.core], self.precv.at[grp, k], self.partner)
 
     def sum_part(self, grp, k):
         mine = self.precv.at[grp, k]
         self.arrive(grp, 13 + k, mine, self.partner)
-        total = self.pbuf[grp, k, self.core].astype(F32) + mine[...].astype(F32)
+        total = self.pbuf[k, self.core].astype(F32) + mine[...].astype(F32)
         mine[...] = total.astype(BF16)
         first, second = mine.at[pl.ds(0, self.half), :], mine.at[pl.ds(self.half, self.half), :]
         if k == 0:
@@ -145,14 +145,17 @@
         self.arrive(grp, 21, self.r_near.at[grp, 0, low, :], self.left)
         self.arrive(grp, 22, self.r_near.at[grp, 1, high, :], self.right)
         total = self.precv[grp, 3].astype(F32) + self.r_near[grp, 0].astype(F32) + self.r_near[grp, 1].astype(F32)
-        self.out[grp] = total.astype(BF16)
+        return total.astype(BF16).astype(F32)
+
+    def settle(self, grp, idx):
+        self.sent.pop((grp, idx)).wait_send()
 
     def drain(self):
-        for desc in self.sent:
+        for desc in self.sent.values():
             desc.wait_send()
 
 
-def run_schedule(ring, stages, part_dot, on_full, head=((), (), ()), tail=((), (), ())):
+def run_schedule(ring, stages, part_dot, on_full, epilogue, head=((), (), ()), tail=((), (), ())):
     def fill(work):
         for fn in work:
             fn()
@@ -166,9 +169,11 @@
         def column(step, carry):
             cols = pl.ds(pl.multiple_of(step * tile, tile), tile)
             val = part_dot(grp, row0, 2 * rows, step * tile, tile).astype(BF16)
-            ring.pbuf[grp, k, 0, :, cols] = val[:rows]
-            ring.pbuf[grp, k, 1, :, cols] = val[rows:]
+            ring.pbuf[k, 0, :, cols] = val[:rows]
+            ring.pbuf[k, 1, :, cols] = val[rows:]
             return carry
+        if grp > 0:
+            ring.settle(grp - 1, 13 + k)
         lax.fori_loop(0, 3, column, 0)
         ring.send_part(grp, k)
 
@@ -212,13 +217,74 @@
     parts(1, 3)
     ring.sum_part(1, 2)
     fill(tail[0])
-    ring.finish(0)
+    epilogue(0, ring.finish(0))
     ring.sum_part(1, 3)
     fill(tail[1])
     ring.relay(1)
     fill(tail[2])
-    ring.finish(1)
+    epilogue(1, ring.finish(1))
     ring.drain()
+
+
+def add_norm(base_hbm, vecs, rows_of, hid_hbm, out, base, sem, saves):
+    add_row, gain_row, shift_row = rows_of
+    load = pltpu.make_async_copy(base_hbm, base, sem.at[8])
+    load.start()
+
+    def vec(row):
+        return vecs[row[0], pl.ds(row[1], 1), :]
+
+    def epilogue(grp, total):
+        if grp == 0:
+            load.wait()
+        val = base[grp] + total + vec(add_row)
+        base[grp] = val
+        store = pltpu.make_async_copy(base.at[grp], hid_hbm.at[grp], sem.at[9 + grp])
+        store.start()
+        saves.append(store)
+        out[grp] = layer_norm(val, vec(gain_row), vec(shift_row)).astype(BF16)
+    return epilogue
+
+
+class NormGrad:
+    def __init__(self, base_hbm, dres_hbm, vecs, gain_row, new_hbm, out, vgrad, base, dres, new, sem):
+        self.base_hbm, self.dres_hbm, self.new_hbm = base_hbm, dres_hbm, new_hbm
+        self.vecs, self.gain_row, self.out, self.vgrad = vecs, gain_row, out, vgrad
+        self.base, self.dres, self.new, self.sem = base, dres, new, sem
+        self.store = None
+        vgrad[...] = jnp.zeros_like(vgrad)
+        self.load(0)
+
+    def load(self, grp):
+        self.loads = [pltpu.make_async_copy(self.base_hbm.at[grp], self.base, self.sem.at[0]),
+                      pltpu.make_async_copy(self.dres_hbm.at[grp], self.dres, self.sem.at[1])]
+        for copy in self.loads:
+            copy.start()
+
+    def __call__(self, grp, d_norm):
+        for copy in self.loads:
+            copy.wait()
+        x_val, d_res = self.base[...], self.dres[...]
+        centered = x_val - jnp.mean(x_val, axis=-1, keepdims=True)
+        inv_std = lax.rsqrt(jnp.mean(centered * centered, axis=-1, keepdims=True) + 1e-5)
+        x_hat = centered * inv_std
+        d_hat = d_norm * self.vecs[self.gain_row[0], pl.ds(self.gain_row[1], 1), :]
+        mean_d = jnp.mean(d_hat, axis=-1, keepdims=True)
+        mean_dx = jnp.mean(d_hat * x_hat, axis=-1, keepdims=True)
+        d_new = d_res + inv_std * (d_hat - mean_d - x_hat * mean_dx)
+        for row, val in enumerate((d_norm * x_hat, d_norm, d_new, d_res)):
+            self.vgrad[pl.ds(row, 1), :] += jnp.sum(val, axis=0, keepdims=True)
+        if self.store is not None:
+            self.store.wait()
+        self.new[...] = d_new
+        self.out[grp] = d_new.astype(BF16)
+        self.store = pltpu.make_async_copy(self.new, self.new_hbm.at[grp], self.sem.at[2])
+        self.store.start()
+        if grp + 1 < GROUPS:
+            self.load(grp + 1)
+
+    def drain(self):
+        self.store.wait()
 
 
 def row_blocks(n_rows, block, body):
@@ -284,13 +350,14 @@
     ref[grp, :, seq, :, head * LANES:(head + 1) * LANES] = val.reshape(n_dev, pos, LANES)
 
 
-def attn_fwd_kernel(n_dev, n_heads, scale, src, lengths, w_in, w_out, out, full_out, qkv_out, ctx_out,
-                    full, qkv, ctx, w_in_v, w_out_v, pbuf, precv, r_far, r_near, send_sem, recv_sem, own_sem, local_sem):
+def attn_fwd_kernel(n_dev, n_heads, scale, layer, rows_of, src, lengths, w_in, w_out, base, vecs, out, hid, full_out, qkv_out, ctx_out,
+                    full, qkv, ctx, w_in_v, w_out_v, e_base, pbuf, precv, r_far, r_near, send_sem, recv_sem, own_sem, local_sem):
     ring = Ring(n_dev, src, full, pbuf, precv, r_far, r_near, out, send_sem, recv_sem, own_sem)
     ring.barrier()
-    load_in = load_heads(w_in, w_in_v, local_sem.at[0], True)
-    load_out = load_heads(w_out, w_out_v, local_sem.at[1], True)
+    load_in = load_heads(w_in.at[layer], w_in_v, local_sem.at[0], True)
+    load_out = load_heads(w_out.at[layer], w_out_v, local_sem.at[1], True)
     saves = []
+    epilogue = add_norm(base, vecs, rows_of, hid, out, e_base, local_sem, saves)
     n_seq, pos = qkv.shape[2], qkv.shape[3]
     n_rows, d_model = full.shape[1], full.shape[2]
     shard_rows = n_seq * pos
@@ -333,13 +400,13 @@
         w_cols = w_out_v[:, :, pl.ds(pl.multiple_of(col0, tile), tile)].reshape(n_heads * LANES, tile)
         return dot_nn(lhs, w_cols)
 
-    run_schedule(ring, stages, part_dot, on_full)
+    run_schedule(ring, stages, part_dot, on_full, epilogue)
     for copy in saves:
         copy.wait()
 
 
-def attn_bwd_kernel(n_dev, n_heads, scale, src, lengths, w_in, w_out, qkv_hbm, ctx_hbm, a_hbm, m_hbm, dpre_hbm,
-                    out, g_in, g_out, g_up, full, act, qkv, dctx, dqkv, w_in_v, w_out_v, stage, stage_sem,
+def attn_bwd_kernel(n_dev, n_heads, scale, layer, src, lengths, w_in, w_out, qkv_hbm, ctx_hbm, a_hbm, m_hbm, dpre_hbm, base_hbm, dres_hbm, vecs,
+                    out, new_hbm, vgrad, g_in, g_out, g_up, full, act, qkv, dctx, dqkv, w_in_v, w_out_v, stage, stage_sem, e_base, e_dres, e_new, e_sem,
                      pbuf, precv, r_far, r_near, send_sem, recv_sem, own_sem, local_sem):
     ring = Ring(n_dev, src, full, pbuf, precv, r_far, r_near, out, send_sem, recv_sem, own_sem)
     ring.barrier()
@@ -348,23 +415,27 @@
     load_dpre = pltpu.make_async_copy(dpre_hbm, dqkv, local_sem.at[3])
     load_dpre.start()
     load_m.start()
-    load_out = load_heads(w_out, w_out_v, local_sem.at[1], True)
     load_qkv = pltpu.make_async_copy(qkv_hbm, qkv, local_sem.at[6])
     load_ctx = pltpu.make_async_copy(ctx_hbm, dctx, local_sem.at[4])
-    load_qkv.start()
-    load_in = load_heads(w_in, w_in_v, local_sem.at[0], True)
+    late = []
+
+    def late_loads():
+        late.append(load_heads(w_out.at[layer], w_out_v, local_sem.at[1], True))
+        load_qkv.start()
+        late.append(load_qkv)
+        late.append(load_heads(w_in.at[layer], w_in_v, local_sem.at[0], True))
+    epilogue = NormGrad(base_hbm, dres_hbm, vecs, (layer, 0), new_hbm, out, vgrad, e_base, e_dres, e_new, e_sem)
     load_a = pltpu.make_async_copy(a_hbm, act, local_sem.at[5])
     n_seq, pos = qkv.shape[2], qkv.shape[3]
     n_rows, d_model = full.shape[1], full.shape[2]
     shard_rows = n_seq * pos
     tile = n_heads * LANES
-    head_dim = w_out.shape[1]
+    head_dim = w_out.shape[2]
 
     def on_full(grp):
         if grp == 0:
-            load_in.wait()
-            load_out.wait()
-            load_qkv.wait()
+            for copy in late:
+                copy.wait()
             load_a.start()
 
     def stages(grp):
@@ -432,24 +503,26 @@
 
     n_up = d_model // tile
     ups = [up_tile(step) for step in range(n_up)]
-    head = (ups[:n_up // 3], ups[n_up // 3:2 * (n_up // 3)], ups[2 * (n_up // 3):])
-    run_schedule(ring, stages, part_dot, on_full, head, ([out_grad], [in_tile(0)], [in_tile(1), in_tile(2)]))
+    head = ([], [late_loads] + ups[:n_up // 2], ups[n_up // 2:])
+    run_schedule(ring, stages, part_dot, on_full, epilogue, head, ([out_grad], [in_tile(0)], [in_tile(1), in_tile(2)]))
     stager.drain()
+    epilogue.drain()
 
 
 def gelu_tanh(pre_act):
     return jax.nn.gelu(pre_act, approximate=True)
 
 
-def mlp_fwd_kernel(n_dev, src, w_up, b_up, w_down, out, full_out, pre_out,
-                   full, pre, act, w_up_v, w_down_v, pbuf, precv, r_far, r_near, send_sem, recv_sem, own_sem, local_sem):
+def mlp_fwd_kernel(n_dev, layer, rows_of, src, w_up, b_up, w_down, base, vecs, out, hid, full_out, pre_out,
+                   full, pre, act, w_up_v, w_down_v, e_base, pbuf, precv, r_far, r_near, send_sem, recv_sem, own_sem, local_sem):
     ring = Ring(n_dev, src, full, pbuf, precv, r_far, r_near, out, send_sem, recv_sem, own_sem)
     ring.barrier()
-    load_in = pltpu.make_async_copy(w_up, w_up_v, local_sem.at[0])
-    load_out = pltpu.make_async_copy(w_down, w_down_v, local_sem.at[1])
+    load_in = pltpu.make_async_copy(w_up.at[layer], w_up_v, local_sem.at[0])
+    load_out = pltpu.make_async_copy(w_down.at[layer], w_down_v, local_sem.at[1])
     load_in.start()
     load_out.start()
     saves = []
+    epilogue = add_norm(base, vecs, rows_of, hid, out, e_base, local_sem, saves)
     n_rows = full.shape[1]
     block = 2 * ring.rows
 
@@ -478,7 +551,7 @@
     def part_dot(grp, row0, rows, col0, tile):
         return dot_nn(act[grp, pl.ds(row0, rows), :], w_down_v[:, pl.ds(pl.multiple_of(col0, tile), tile)])
 
-    run_schedule(ring, stages, part_dot, on_full)
+    run_schedule(ring, stages, part_dot, on_full, epilogue)
     for copy in saves:
         copy.wait()
 
@@ -492,17 +565,18 @@
     return pre_act * cdf, grad * (cdf + 0.5 * pre_act * (1.0 - tanh_val * tanh_val) * slope)
 
 
-def mlp_bwd_kernel(n_dev, src, w_up, w_down, pre_hbm, out, dpre_out, dbias_out, g_down,
-                   full, pre, act, dpre, w_up_v, w_down_v, stage, stage_sem,
+def mlp_bwd_kernel(n_dev, layer, src, w_up, w_down, pre_hbm, base_hbm, dres_hbm, vecs, out, new_hbm, vgrad, dpre_out, dbias_out, g_down,
+                   full, pre, act, dpre, w_up_v, w_down_v, stage, stage_sem, e_base, e_dres, e_new, e_sem,
                    pbuf, precv, r_far, r_near, send_sem, recv_sem, own_sem, local_sem):
     ring = Ring(n_dev, src, full, pbuf, precv, r_far, r_near, out, send_sem, recv_sem, own_sem)
     ring.barrier()
     stager = Stager(stage, stage_sem.at[0])
-    load_in = pltpu.make_async_copy(w_up, w_up_v, local_sem.at[0])
-    load_out = pltpu.make_async_copy(w_down, w_down_v, local_sem.at[1])
+    load_in = pltpu.make_async_copy(w_up.at[layer], w_up_v, local_sem.at[0])
+    load_out = pltpu.make_async_copy(w_down.at[layer], w_down_v, local_sem.at[1])
     load_pre = [pltpu.make_async_copy(pre_hbm.at[grp], pre, local_sem.at[2 + grp]) for grp in range(GROUPS)]
     for copy in (load_out, load_pre[0], load_in):
         copy.start()
+    epilogue = NormGrad(base_hbm, dres_hbm, vecs, (layer, 2), new_hbm, out, vgrad, e_base, e_dres, e_new, e_sem)
     dbias_out[...] = jnp.zeros_like(dbias_out)
     saves = []
     n_rows = full.shape[1]
@@ -543,17 +617,18 @@
                         for lanes in (slice(0, half), slice(half, 2 * half))], lambda ref: ref, g_down.at[cols, :])
         return run
 
-    run_schedule(ring, stages, part_dot, on_full, tail=([down_tile(0)], [down_tile(1)], [down_tile(2)]))
+    run_schedule(ring, stages, part_dot, on_full, epilogue, tail=([down_tile(0)], [down_tile(1)], [down_tile(2)]))
     stager.drain()
+    epilogue.drain()
     for copy in saves:
         copy.wait()
 
 
 def ring_scratch(n_dev, rows, d_model):
-    return [pltpu.VMEM((GROUPS, 4, 2, rows, d_model), BF16), pltpu.VMEM((GROUPS, 4, rows, d_model), BF16),
+    return [pltpu.VMEM((4, 2, rows, d_model), BF16), pltpu.VMEM((GROUPS, 4, rows, d_model), BF16),
             pltpu.VMEM((GROUPS, 2, rows // 2, d_model), BF16), pltpu.VMEM((GROUPS, 2, rows, d_model), BF16),
             pltpu.SemaphoreType.DMA((GROUPS, N_COPIES)), pltpu.SemaphoreType.DMA((GROUPS, N_COPIES)),
-            pltpu.SemaphoreType.DMA((GROUPS,)), pltpu.SemaphoreType.DMA((8,))]
+            pltpu.SemaphoreType.DMA((GROUPS,)), pltpu.SemaphoreType.DMA((12,))]
 
 
 def call_kernel(kernel, name, collective_id, out_shape, out_specs, in_specs, scratch, flops, args):
@@ -567,64 +642,98 @@
     return jax.ShapeDtypeStruct(dims, dtype)
 
 
-def dims_of(shard, n_dev):
-    n_seq, pos, d_model = shard.shape[0] // GROUPS, shard.shape[1], shard.shape[2]
-    return n_seq, pos, n_seq * pos, n_dev * n_seq * pos, d_model
-
-
-def attn_fwd(shard, lengths, w_in, w_out, n_dev, collective_id):
-    n_seq, pos, rows, n_rows, d_model = dims_of(shard, n_dev)
-    n_heads, head_dim = w_out.shape[0], w_out.shape[1]
-    n_cols, c_cols = w_in.shape[0] * LANES, n_heads * LANES
+def dims_of(shard, seq_pos, n_dev):
+    rows, d_model = shard.shape[1], shard.shape[2]
+    return rows // seq_pos, seq_pos, rows, n_dev * rows, d_model
+
+
+def attn_fwd(layer, rows_of, shard, base, vecs, pos, lengths, w_in, w_out, n_dev, collective_id):
+    n_seq, pos, rows, n_rows, d_model = dims_of(shard, pos, n_dev)
+    n_heads, head_dim = w_out.shape[1], w_out.shape[2]
+    n_cols, c_cols = w_in.shape[1] * LANES, n_heads * LANES
     qkv_dims, ctx_dims = (GROUPS, n_dev, n_seq, pos, n_cols), (GROUPS, n_dev, n_seq, pos, c_cols)
-    out, full, qkv, ctx = call_kernel(
-        functools.partial(attn_fwd_kernel, n_dev, n_heads, head_dim ** -0.5), 'attn_fwd', collective_id,
-        (shape((GROUPS, rows, d_model), BF16), shape((GROUPS, n_rows, d_model), BF16), shape(qkv_dims, BF16), shape(ctx_dims, BF16)),
-        (VMEM, ANY, ANY, ANY), (VMEM, SMEM, ANY, ANY),
+    return call_kernel(
+        functools.partial(attn_fwd_kernel, n_dev, n_heads, head_dim ** -0.5, layer, rows_of), 'attn_fwd', collective_id,
+        (shape(shard.shape, BF16), shape(shard.shape, F32), shape((GROUPS, n_rows, d_model), BF16), shape(qkv_dims, BF16), shape(ctx_dims, BF16)),
+        (VMEM, ANY, ANY, ANY, ANY), (VMEM, SMEM, ANY, ANY, ANY, VMEM),
         [pltpu.VMEM((GROUPS, n_rows, d_model), BF16), pltpu.VMEM(qkv_dims, BF16), pltpu.VMEM(ctx_dims, BF16),
-         pltpu.VMEM((w_in.shape[0], LANES, d_model), BF16), pltpu.VMEM((n_heads, LANES, d_model), BF16)] + ring_scratch(n_dev, rows, d_model),
-        2 * GROUPS * n_rows * d_model * (n_cols + c_cols), (shard.reshape(GROUPS, rows, d_model), lengths, w_in, w_out))
-    return out.reshape(shard.shape), full, qkv, ctx
-
-
-def attn_bwd(shard, lengths, w_in, w_out, qkv, ctx, a_full, m_full, dpre, n_dev, collective_id):
-    n_seq, pos, rows, n_rows, d_model = dims_of(shard, n_dev)
-    n_heads, head_dim = w_out.shape[0], w_out.shape[1]
-    n_cols, c_cols, ff = w_in.shape[0] * LANES, n_heads * LANES, dpre.shape[2]
+         pltpu.VMEM((w_in.shape[1], LANES, d_model), BF16), pltpu.VMEM((n_heads, LANES, d_model), BF16), pltpu.VMEM(base.shape, F32)] + ring_scratch(n_dev, rows, d_model),
+        2 * GROUPS * n_rows * d_model * (n_cols + c_cols), (shard, lengths, w_in, w_out, base, vecs))
+
+
+def mlp_fwd(layer, rows_of, shard, base, vecs, pos, w_up, b_up, w_down, n_dev, collective_id):
+    n_seq, pos, rows, n_rows, d_model = dims_of(shard, pos, n_dev)
+    ff = w_up.shape[2]
     return call_kernel(
-        functools.partial(attn_bwd_kernel, n_dev, n_heads, head_dim ** -0.5), 'attn_bwd', collective_id,
-        (shape((GROUPS, rows, d_model), BF16), shape(w_in.shape, BF16), shape(w_out.shape, BF16), shape((d_model // LANES, LANES, ff), BF16)),
-        (VMEM, ANY, ANY, ANY), (VMEM, SMEM) + (ANY,) * 7,
+        functools.partial(mlp_fwd_kernel, n_dev, layer, rows_of), 'mlp_fwd', collective_id,
+        (shape(shard.shape, BF16), shape(shard.shape, F32), shape((GROUPS, n_rows, d_model), BF16), shape((GROUPS, n_rows, ff), F32)),
+        (VMEM, ANY, ANY, ANY), (VMEM, ANY, VMEM, ANY, ANY, VMEM),
+        [pltpu.VMEM((GROUPS, n_rows, d_model), BF16), pltpu.VMEM((GROUPS, n_rows, ff), F32), pltpu.VMEM((GROUPS, n_rows, ff), BF16),
+         pltpu.VMEM(w_up.shape[1:], BF16), pltpu.VMEM(w_down.shape[1:], BF16), pltpu.VMEM(base.shape, F32)] + ring_scratch(n_dev, rows, d_model),
+        4 * GROUPS * n_rows * d_model * ff, (shard, w_up, b_up[layer].reshape(1, ff), w_down, base, vecs))
+
+
+def norm_grad_scratch(rows, d_model):
+    return [pltpu.VMEM((rows, d_model), F32)] * 3 + [pltpu.SemaphoreType.DMA((3,))]
+
+
+def attn_bwd(layer, shard, base, d_res, vecs, pos, lengths, w_in, w_out, qkv, ctx, a_full, m_full, dpre, n_dev, collective_id):
+    n_seq, pos, rows, n_rows, d_model = dims_of(shard, pos, n_dev)
+    n_heads, head_dim = w_out.shape[1], w_out.shape[2]
+    n_cols, c_cols, ff = w_in.shape[1] * LANES, n_heads * LANES, dpre.shape[2]
+    return call_kernel(
+        functools.partial(attn_bwd_kernel, n_dev, n_heads, head_dim ** -0.5, layer), 'attn_bwd', collective_id,
+        (shape(shard.shape, BF16), shape(shard.shape, F32), shape((4, d_model), F32),
+         shape(w_in.shape[1:], BF16), shape(w_out.shape[1:], BF16), shape((d_model // LANES, LANES, ff), BF16)),
+        (VMEM, ANY, VMEM, ANY, ANY, ANY), (VMEM, SMEM) + (ANY,) * 9 + (VMEM,),
         [pltpu.VMEM((GROUPS, n_rows, d_model), BF16), pltpu.VMEM((GROUPS, n_rows, d_model), BF16),
          pltpu.VMEM(qkv.shape, BF16), pltpu.VMEM(ctx.shape, BF16), pltpu.VMEM(qkv.shape, BF16),
-         pltpu.VMEM((w_in.shape[0], LANES, d_model), BF16), pltpu.VMEM((n_heads, LANES, d_model), BF16),
-         pltpu.VMEM((2, n_heads, LANES, d_model), BF16), pltpu.SemaphoreType.DMA((1, 2))] + ring_scratch(n_dev, rows, d_model),
-        4 * GROUPS * n_rows * d_model * (n_cols + c_cols), (shard.reshape(GROUPS, rows, d_model), lengths, w_in, w_out, qkv, ctx, a_full, m_full, dpre.reshape(qkv.shape)))
-
-
-def mlp_fwd(shard, w_up, b_up, w_down, n_dev, collective_id):
-    n_seq, pos, rows, n_rows, d_model = dims_of(shard, n_dev)
-    ff = w_up.shape[1]
-    out, full, pre = call_kernel(
-        functools.partial(mlp_fwd_kernel, n_dev), 'mlp_fwd', collective_id,
-        (shape((GROUPS, rows, d_model), BF16), shape((GROUPS, n_rows, d_model), BF16), shape((GROUPS, n_rows, ff), F32)),
-        (VMEM, ANY, ANY), (VMEM, ANY, VMEM, ANY),
-        [pltpu.VMEM((GROUPS, n_rows, d_model), BF16), pltpu.VMEM((GROUPS, n_rows, ff), F32), pltpu.VMEM((GROUPS, n_rows, ff), BF16),
-         pltpu.VMEM(w_up.shape, BF16), pltpu.VMEM(w_down.shape, BF16)] + ring_scratch(n_dev, rows, d_model),
-        4 * GROUPS * n_rows * d_model * ff, (shard.reshape(GROUPS, rows, d_model), w_up, b_up.reshape(1, ff), w_down))
-    return out.reshape(shard.shape), full, pre
-
-
-def mlp_bwd(shard, w_up, w_down, pre, n_dev, collective_id):
-    n_seq, pos, rows, n_rows, d_model = dims_of(shard, n_dev)
-    ff = w_up.shape[1]
+         pltpu.VMEM((w_in.shape[1], LANES, d_model), BF16), pltpu.VMEM((n_heads, LANES, d_model), BF16),
+         pltpu.VMEM((2, n_heads, LANES, d_model), BF16), pltpu.SemaphoreType.DMA((1, 2))] + norm_grad_scratch(rows, d_model) + ring_scratch(n_dev, rows, d_model),
+        4 * GROUPS * n_rows * d_model * (n_cols + c_cols),
+        (shard, lengths, w_in, w_out, qkv, ctx, a_full, m_full, dpre.reshape(qkv.shape), base, d_res, vecs))
+
+
+def mlp_bwd(layer, shard, base, d_res, vecs, pos, w_up, w_down, pre, n_dev, collective_id):
+    n_seq, pos, rows, n_rows, d_model = dims_of(shard, pos, n_dev)
+    ff = w_up.shape[2]
     return call_kernel(
-        functools.partial(mlp_bwd_kernel, n_dev), 'mlp_bwd', collective_id,
-        (shape((GROUPS, rows, d_model), BF16), shape((GROUPS, n_rows, ff), BF16), shape((1, ff), F32), shape(w_down.shape, BF16)),
-        (VMEM, ANY, VMEM, ANY), (VMEM, ANY, ANY, ANY),
+        functools.partial(mlp_bwd_kernel, n_dev, layer), 'mlp_bwd', collective_id,
+        (shape(shard.shape, BF16), shape(shard.shape, F32), shape((4, d_model), F32),
+         shape((GROUPS, n_rows, ff), BF16), shape((1, ff), F32), shape(w_down.shape[1:], BF16)),
+        (VMEM, ANY, VMEM, ANY, VMEM, ANY), (VMEM,) + (ANY,) * 5 + (VMEM,),
         [pltpu.VMEM((GROUPS, n_rows, d_model), BF16), pltpu.VMEM((n_rows, ff), F32), pltpu.VMEM((GROUPS, n_rows, ff), BF16), pltpu.VMEM((GROUPS, n_rows, ff), BF16),
-         pltpu.VMEM(w_up.shape, BF16), pltpu.VMEM(w_down.shape, BF16), pltpu.VMEM((2, ff // 3, d_model), BF16), pltpu.SemaphoreType.DMA((1, 2))] + ring_scratch(n_dev, rows, d_model),
-        6 * GROUPS * n_rows * d_model * ff, (shard.reshape(GROUPS, rows, d_model), w_up, w_down, pre))
+         pltpu.VMEM(w_up.shape[1:], BF16), pltpu.VMEM(w_down.shape[1:], BF16), pltpu.VMEM((2, ff // 3, d_model), BF16),
+         pltpu.SemaphoreType.DMA((1, 2))] + norm_grad_scratch(rows, d_model) + ring_scratch(n_dev, rows, d_model),
+        6 * GROUPS * n_rows * d_model * ff, (shard, w_up, w_down, pre, base, d_res, vecs))
+
+
+def stack_kernel(n_layers, n_arrays, *refs):
+    n_in = n_layers * n_arrays
+    ins, outs, bufs = refs[:n_in], refs[n_in:n_in + n_arrays], refs[n_in + n_arrays:n_in + 2 * n_arrays]
+    load_sem, store_sem = refs[n_in + 2 * n_arrays:]
+    pairs = [(pos, layer) for pos in range(n_arrays) for layer in range(n_layers)]
+    loads = [pltpu.make_async_copy(ins[layer * n_arrays + pos], bufs[pos].at[layer], load_sem.at[idx]) for idx, (pos, layer) in enumerate(pairs)]
+    stores = [pltpu.make_async_copy(bufs[pos].at[layer], outs[pos].at[layer], store_sem.at[idx]) for idx, (pos, layer) in enumerate(pairs)]
+    for copy in loads:
+        copy.start()
+    for load, store in zip(loads, stores):
+        load.wait()
+        store.start()
+    for copy in stores:
+        copy.wait()
+
+
+def stack_layers(layer_arrays):
+    n_layers, n_arrays = len(layer_arrays), len(layer_arrays[0])
+    shapes = [(n_layers,) + val.shape for val in layer_arrays[0]]
+    flat = [val for arrays in layer_arrays for val in arrays]
+    return pl.pallas_call(
+        functools.partial(stack_kernel, n_layers, n_arrays), out_shape=tuple(shape(dims, BF16) for dims in shapes),
+        in_specs=[ANY] * len(flat), out_specs=(ANY,) * n_arrays, name='stack_layers',
+        scratch_shapes=[pltpu.VMEM(dims, BF16) for dims in shapes] + [pltpu.SemaphoreType.DMA((len(flat),)), pltpu.SemaphoreType.DMA((len(flat),))],
+        cost_estimate=pl.CostEstimate(flops=0, bytes_accessed=100_000_000, transcendentals=0),
+        compiler_params=pltpu.CompilerParams(vmem_limit_bytes=VMEM_LIMIT))(*flat)
 
 
 def sum_kernel(n_dev, parts, out, landed, total, send_sem, recv_sem):
@@ -676,49 +785,38 @@
     return centered * lax.rsqrt(row_var + 1e-5) * gain_vec + shift_vec
 
 
-def layer_fwd(x_cur, lengths, weights, vec_layer, n_dev, collective_id):
-    w_in, w_out, w_up, b_up, w_down = weights
-    a_shard = layer_norm(x_cur, vec_layer[0], vec_layer[1]).astype(BF16)
-    attn_shard, a_full, qkv, ctx = attn_fwd(a_shard, lengths, w_in, w_out, n_dev, collective_id)
-    hidden = x_cur + attn_shard.astype(F32) + vec_layer[4]
-    m_shard = layer_norm(hidden, vec_layer[2], vec_layer[3]).astype(BF16)
-    mlp_shard, m_full, pre = mlp_fwd(m_shard, w_up, b_up, w_down, n_dev, collective_id + 1)
-    x_next = hidden + mlp_shard.astype(F32) + vec_layer[5]
-    return x_next, (x_cur, a_full, qkv, ctx, hidden, m_full, pre)
-
-
-def layer_bwd(d_cur, residues, lengths, weights, vec_layer, n_dev, collective_id):
-    w_in, w_out, w_up, _, w_down = weights
-    x_prev, a_full, qkv, ctx, hidden, m_full, pre = residues
-    n_heads, head_dim, d_model = w_out.shape
-    d_mid, d_pre, g_bup, g_down = mlp_bwd(d_cur.astype(BF16), w_up, w_down, pre, n_dev, collective_id)
-    d_hid_ln, d_gain2, d_shift2 = jax.vjp(layer_norm, hidden, vec_layer[2], vec_layer[3])[1](d_mid.reshape(d_cur.shape).astype(F32))
-    d_hid = d_cur + d_hid_ln
-    d_in, g_in, g_out, g_up = attn_bwd(d_hid.astype(BF16), lengths, w_in, w_out, qkv, ctx, a_full, m_full, d_pre, n_dev, collective_id + 1)
-    d_x_ln, d_gain1, d_shift1 = jax.vjp(layer_norm, x_prev, vec_layer[0], vec_layer[1])[1](d_in.reshape(d_cur.shape).astype(F32))
-    g_vec = jnp.stack([d_gain1, d_shift1, d_gain2, d_shift2, jnp.sum(d_hid, axis=(0, 1)), jnp.sum(d_cur, axis=(0, 1))])
-    return d_hid + d_x_ln, (g_in, g_out, g_up.reshape(w_up.shape), g_bup[0], g_down, g_vec)
-
-
 def group_body(n_dev, x_loc, dy_loc, len_loc, wqkv_loc, wout_loc, wup_loc, bup_loc, wdown_loc, vec_loc):
     n_layers, d_model, n_kinds, n_heads, head_dim = wqkv_loc.shape
     w_in_all = jnp.transpose(wqkv_loc, (0, 2, 3, 4, 1)).reshape(n_layers, n_kinds * n_heads, head_dim, d_model)
-    saved_acts = []
-    x_cur = x_loc
-    weights_of = lambda idx: (w_in_all[idx], wout_loc[idx], wup_loc[idx], bup_loc[idx], wdown_loc[idx])
-    for layer_idx in range(n_layers):
-        x_cur, residues = layer_fwd(x_cur, len_loc, weights_of(layer_idx), vec_loc[layer_idx], n_dev, 2 * layer_idx)
-        saved_acts.append(residues)
-    d_cur = dy_loc.astype(F32)
-    layer_grads = [None] * n_layers
-    for layer_idx in reversed(range(n_layers)):
-        d_cur, grad_set = layer_bwd(d_cur, saved_acts[layer_idx], len_loc, weights_of(layer_idx), vec_loc[layer_idx], n_dev,
-                                    2 * n_layers + 2 * layer_idx)
-        layer_grads[layer_idx] = grad_set
-    stacked = [jnp.stack([grad_set[grad_pos] for grad_set in layer_grads]) for grad_pos in range(6)]
-    g_vec = sum_over_devices(stacked[5], n_dev, 4 * n_layers)
-    g_qkv = jnp.transpose(stacked[0].reshape(n_layers, n_kinds, n_heads, head_dim, d_model), (0, 4, 1, 2, 3))
-    return x_cur, d_cur, g_qkv, stacked[1], stacked[2], stacked[3], stacked[4], g_vec
+    pos = x_loc.shape[1]
+    rows_shape = (GROUPS, x_loc.shape[0] // GROUPS * pos, d_model)
+    x_cur = x_loc.reshape(rows_shape)
+    shard = layer_norm(x_cur, vec_loc[0, 0], vec_loc[0, 1]).astype(BF16)
+    saved = []
+    for layer in range(n_layers):
+        after = min(layer + 1, n_layers - 1)
+        mid_shard, hidden, a_full, qkv, ctx = attn_fwd(layer, ((layer, 4), (layer, 2), (layer, 3)), shard, x_cur, vec_loc, pos, len_loc,
+                                                       w_in_all, wout_loc, n_dev, 2 * layer)
+        shard, x_next, m_full, pre = mlp_fwd(layer, ((layer, 5), (after, 0), (after, 1)), mid_shard, hidden, vec_loc, pos,
+                                             wup_loc, bup_loc, wdown_loc, n_dev, 2 * layer + 1)
+        saved.append((x_cur, a_full, qkv, ctx, hidden, m_full, pre))
+        x_cur = x_next
+    shard = dy_loc.reshape(rows_shape)
+    d_cur = shard.astype(F32)
+    layer_grads, small_grads = [None] * n_layers, [None] * n_layers
+    for layer in reversed(range(n_layers)):
+        x_prev, a_full, qkv, ctx, hidden, m_full, pre = saved[layer]
+        first_id = 2 * n_layers + 2 * layer
+        mid_shard, d_hid, v_mlp, d_pre, g_bup, g_down = mlp_bwd(layer, shard, hidden, d_cur, vec_loc, pos, wup_loc, wdown_loc, pre, n_dev, first_id)
+        shard, d_cur, v_attn, g_in, g_out, g_up = attn_bwd(layer, mid_shard, x_prev, d_hid, vec_loc, pos, len_loc, w_in_all, wout_loc,
+                                                           qkv, ctx, a_full, m_full, d_pre, n_dev, first_id + 1)
+        layer_grads[layer] = (g_in, g_out, g_up.reshape(wup_loc.shape[1:]), g_down)
+        small_grads[layer] = (g_bup[0], jnp.concatenate([v_attn[:2], v_mlp]))
+    g_vec = sum_over_devices(jnp.stack([grad_set[1] for grad_set in small_grads]), n_dev, 4 * n_layers)
+    g_bup = jnp.stack([grad_set[0] for grad_set in small_grads])
+    g_in, g_out, g_up, g_down = stack_layers(layer_grads)
+    g_qkv = jnp.transpose(g_in.reshape(n_layers, n_kinds, n_heads, head_dim, d_model), (0, 4, 1, 2, 3))
+    return x_cur.reshape(x_loc.shape), d_cur.reshape(x_loc.shape), g_qkv, g_out, g_up, g_bup, g_down, g_vec
 
 
 def solution(mesh):

time: 1210 us -> 1130 us (0.934)
  other arithmetic: 108 us -> 8.44 us
  Pallas kernels: 1040 us -> 1100 us
  local copies, waits for them, and re-layouts: 50.6 us -> 12.4 us
    reduce_sum x22 -> x0, other arithmetic: 34.7 us -> none  [the longest x17 27.2 us: layer_norm(): return centered * lax.rsqrt(row_var + 1e-05) * gain_vec + shift_vec]
    pallas_call x0 -> x1, Pallas kernels: none -> 31.8 us  [stack_layers(): pl.pallas_call(functools.partial(stack_kernel, n_layers, n_arrays), out_s...]
    pallas_call x12, Pallas kernels: 1030 us -> 1060 us  [call_kernel(): pl.pallas_call(kernel, out_shape=out_shape, in_specs=in_specs, out_specs=...]
    another operation x5 -> x4, other arithmetic: 28.9 us -> 2.98 us  [the longest x3 1.63 us: group_body(): jnp.stack([grad_set[1] for grad_set in small_grads])]
    squeeze x3 -> x0, local copies, waits for them, and re-layouts: 23.5 us -> none  [the longest x1 12.9 us: group_body(): wup_loc[idx]]
    convert_element_type x11 -> x2, other arithmetic: 15.4 us -> 3.08 us  [the longest x1 1.56 us: group_body(): d_cur = shard.astype(F32)]
where the time goes in v2:
time: 1130 us; the launch traced here: 1120 us
  Pallas kernels  1100 us (97%)
  local copies, waits for them, and re-layouts  12.4 us (1%)
    pallas_call x12, Pallas kernels, call_kernel(): pl.pallas_call(kernel, out_shape=out_shape, in_specs=in_specs, out_specs=...  1060 us
    pallas_call x1, Pallas kernels, stack_layers(): pl.pallas_call(functools.partial(stack_kernel, n_layers, n_arrays), out_s...  31.8 us

profile of v2, /device:TPU:113, one launch (start us, length us, event | category | flops | bytes accessed | tf_op | source)
XLA Modules:
  0.0 1125.0 jit_solution(6230685311351105445)
XLA Ops:
  0.6 2.0 reduce_sum.18
  2.7 0.3 copy-done
  3.0 0.4 multiply_reduce_fusion
  3.5 1.4 fusion
  4.9 1.0 slice_reduce_fusion.1
  5.9 1.5 add_convert_fusion.src
  7.5 1.6 bitcast_convert_fusion.dres_hbm
  9.0 86.3 %attn_fwd.3 = (bf16[2,128,2304]{2,1,0:T(8,128)(2,1)}, f32[2,128,2304]{2,1,0:T(8,128)}, bf16[2,1024,2304]{2,1,0:T(8,128)(2,1)}, bf16[2,8,4,32,1152]{4,3,2,1,0:T(8,128)(2,1)}, bf16[2,8,4,32,384]{4,3,2,1,0:T(8,128)(2,1)}) custom-call(bf16[2,128,2304]{2,1,0:T(8,128)(2,1)} %add_convert_fusion.src, s32[8]{0:T(128)} %lengths.11, bf16[3,9,96,2304]{3,2,1,0:T(8,128)(2,1)} %bitcast.38, ...), custom_call_target="tpu_custom_call" | custom-call | flops 14495514624 | bytes 40000000 | tf_op jit(solution)/shard_map/attn_fwd/pallas_call | solution.py:635
  95.3 84.6 %mlp_fwd.3 = (bf16[2,128,2304]{2,1,0:T(8,128)(2,1)}, f32[2,128,2304]{2,1,0:T(8,128)}, bf16[2,1024,2304]{2,1,0:T(8,128)(2,1)}, f32[2,1024,1152]{2,1,0:T(8,128)}) custom-call(bf16[2,128,2304]{2,1,0:T(8,128)(2,1)} %get-tuple-element.73.src, bf16[3,2304,1152]{2,1,0:T(8,128)(2,1)} %w_up.11, f32[1,1152]{1,0:T(1,128)} %get-tuple-element.141.b_up, ...), custom_call_target="tpu_custom_call" | custom-call | flops 21743271936 | bytes 40000000 | tf_op jit(solution)/shard_map/mlp_fwd/pallas_call | solution.py:635
  179.9 84.2 %attn_fwd.4 = (bf16[2,128,2304]{2,1,0:T(8,128)(2,1)}, f32[2,128,2304]{2,1,0:T(8,128)}, bf16[2,1024,2304]{2,1,0:T(8,128)(2,1)}, bf16[2,8,4,32,1152]{4,3,2,1,0:T(8,128)(2,1)}, bf16[2,8,4,32,384]{4,3,2,1,0:T(8,128)(2,1)}) custom-call(bf16[2,128,2304]{2,1,0:T(8,128)(2,1)} %get-tuple-element.75.src, s32[8]{0:T(128)} %lengths.11, ...), custom_call_target="tpu_custom_call" | custom-call | flops 14495514624 | bytes 40000000 | tf_op jit(solution)/shard_map/attn_fwd/pallas_call | solution.py:635
  264.1 84.8 %mlp_fwd.4 = (bf16[2,128,2304]{2,1,0:T(8,128)(2,1)}, f32[2,128,2304]{2,1,0:T(8,128)}, bf16[2,1024,2304]{2,1,0:T(8,128)(2,1)}, f32[2,1024,1152]{2,1,0:T(8,128)}) custom-call(bf16[2,128,2304]{2,1,0:T(8,128)(2,1)} %get-tuple-element.77.src, bf16[3,2304,1152]{2,1,0:T(8,128)(2,1)} %w_up.11, f32[1,1152]{1,0:T(1,128)} %get-tuple-element.142.b_up, ...), custom_call_target="tpu_custom_call" | custom-call | flops 21743271936 | bytes 40000000 | tf_op jit(solution)/shard_map/mlp_fwd/pallas_call | solution.py:635
  349.0 84.0 %attn_fwd.5 = (bf16[2,128,2304]{2,1,0:T(8,128)(2,1)}, f32[2,128,2304]{2,1,0:T(8,128)}, bf16[2,1024,2304]{2,1,0:T(8,128)(2,1)}, bf16[2,8,4,32,1152]{4,3,2,1,0:T(8,128)(2,1)}, bf16[2,8,4,32,384]{4,3,2,1,0:T(8,128)(2,1)}) custom-call(bf16[2,128,2304]{2,1,0:T(8,128)(2,1)} %get-tuple-element.79.src, s32[8]{0:T(128)} %lengths.11, ...), custom_call_target="tpu_custom_call" | custom-call | flops 14495514624 | bytes 40000000 | tf_op jit(solution)/shard_map/attn_fwd/pallas_call | solution.py:635
  433.0 85.0 %mlp_fwd.5 = (bf16[2,128,2304]{2,1,0:T(8,128)(2,1)}, f32[2,128,2304]{2,1,0:T(8,128)}, bf16[2,1024,2304]{2,1,0:T(8,128)(2,1)}, f32[2,1024,1152]{2,1,0:T(8,128)}) custom-call(bf16[2,128,2304]{2,1,0:T(8,128)(2,1)} %get-tuple-element.81.src, bf16[3,2304,1152]{2,1,0:T(8,128)(2,1)} %w_up.11, f32[1,1152]{1,0:T(1,128)} %get-tuple-element.140.b_up, ...), custom_call_target="tpu_custom_call" | custom-call | flops 21743271936 | bytes 40000000 | tf_op jit(solution)/shard_map/mlp_fwd/pallas_call | solution.py:635
  518.0 88.2 %mlp_bwd.3 = (bf16[2,128,2304]{2,1,0:T(8,128)(2,1)}, f32[2,128,2304]{2,1,0:T(8,128)}, f32[4,2304]{1,0:T(4,128)}, bf16[2,1024,1152]{2,1,0:T(8,128)(2,1)}, f32[1,1152]{1,0:T(1,128)}, /*index=5*/bf16[1152,2304]{1,0:T(8,128)(2,1)}) custom-call(bf16[2,128,2304]{2,1,0:T(8,128)(2,1)} %bitcast.35, bf16[3,2304,1152]{2,1,0:T(8,128)(2,1)} %w_up.11, ...), custom_call_target="tpu_custom_call" | custom-call | flops 32614907904 | bytes 40000000 | tf_op jit(solution)/shard_map/mlp_bwd/pallas_call | solution.py:635
  606.3 95.1 %attn_bwd.3 = (bf16[2,128,2304]{2,1,0:T(8,128)(2,1)}, f32[2,128,2304]{2,1,0:T(8,128)}, f32[4,2304]{1,0:T(4,128)}, bf16[9,96,2304]{2,1,0:T(8,128)(2,1)}, bf16[3,9...) custom-call(bf16[2,128,2304]{2,1,0:T(8,128)(2,1)} %get-tuple-element.85.src, s32[8]{0:T(128)} %lengths.11, ...), custom_call_target="tpu_custom_call" | custom-call | flops 28991029248 | bytes 40000000 | tf_op jit(solution)/shard_map/attn_bwd/pallas_call | solution.py:635
  701.4 87.8 %mlp_bwd.4 = (bf16[2,128,2304]{2,1,0:T(8,128)(2,1)}, f32[2,128,2304]{2,1,0:T(8,128)}, f32[4,2304]{1,0:T(4,128)}, bf16[2,1024,1152]{2,1,0:T(8,128)(2,1)}, f32[1,1152]{1,0:T(1,128)}, /*index=5*/bf16[1152,2304]{1,0:T(8,128)(2,1)}) custom-call(bf16[2,128,2304]{2,1,0:T(8,128)(2,1)} %get-tuple-element.92.src, bf16[3,2304,1152]{2,1,0:T(8,128)(2,1)} %w_up.11, ...), custom_call_target="tpu_custom_call" | custom-call | flops 32614907904 | bytes 40000000 | tf_op jit(solution)/shard_map/mlp_bwd/pallas_call | solution.py:635
  789.2 95.3 %attn_bwd.4 = (bf16[2,128,2304]{2,1,0:T(8,128)(2,1)}, f32[2,128,2304]{2,1,0:T(8,128)}, f32[4,2304]{1,0:T(4,128)}, bf16[9,96,2304]{2,1,0:T(8,128)(2,1)}, bf16[3,9...) custom-call(bf16[2,128,2304]{2,1,0:T(8,128)(2,1)} %get-tuple-element.95.src, s32[8]{0:T(128)} %lengths.11, ...), custom_call_target="tpu_custom_call" | custom-call | flops 28991029248 | bytes 40000000 | tf_op jit(solution)/shard_map/attn_bwd/pallas_call | solution.py:635
  884.5 88.1 %mlp_bwd.5 = (bf16[2,128,2304]{2,1,0:T(8,128)(2,1)}, f32[2,128,2304]{2,1,0:T(8,128)}, f32[4,2304]{1,0:T(4,128)}, bf16[2,1024,1152]{2,1,0:T(8,128)(2,1)}, f32[1,1152]{1,0:T(1,128)}, /*index=5*/bf16[1152,2304]{1,0:T(8,128)(2,1)}) custom-call(bf16[2,128,2304]{2,1,0:T(8,128)(2,1)} %get-tuple-element.102.src, bf16[3,2304,1152]{2,1,0:T(8,128)(2,1)} %w_up.11, ...), custom_call_target="tpu_custom_call" | custom-call | flops 32614907904 | bytes 40000000 | tf_op jit(solution)/shard_map/mlp_bwd/pallas_call | solution.py:635
  972.7 95.1 %attn_bwd.5 = (bf16[2,128,2304]{2,1,0:T(8,128)(2,1)}, f32[2,128,2304]{2,1,0:T(8,128)}, f32[4,2304]{1,0:T(4,128)}, bf16[9,96,2304]{2,1,0:T(8,128)(2,1)}, bf16[3,9...) custom-call(bf16[2,128,2304]{2,1,0:T(8,128)(2,1)} %get-tuple-element.105.src, s32[8]{0:T(128)} %lengths.11, ...), custom_call_target="tpu_custom_call" | custom-call | flops 28991029248 | bytes 40000000 | tf_op jit(solution)/shard_map/attn_bwd/pallas_call | solution.py:635
  1067.8 1.3 pad_maximum_fusion.1
  1069.1 0.8 slice.32
  1069.9 0.8 slice.33
  1070.7 0.8 slice.34
  1071.5 0.8 maximum_bitcast_fusion.2
  1072.2 0.8 maximum_bitcast_fusion
  1073.2 0.7 reshape.106.parts
  1073.8 12.4 %sum_devices.1 = f32[8,41,128]{2,1,0:T(8,128)} custom-call(f32[8,41,128]{2,1,0:T(8,128)} %reshape.106.parts), custom_call_target="tpu_custom_call" | custom-call | tf_op jit(solution)/shard_map/sum_devices/pallas_call | solution.py:773
  1086.3 0.9 reshape.107
  1087.2 0.7 reshape.108
  1087.9 31.8 %stack_layers.1 = (bf16[3,9,96,2304]{3,2,1,0:T(8,128)(2,1)}, bf16[3,3,96,2304]{3,2,1,0:T(8,128)(2,1)}, bf16[3,2304,1152]{2,1,0:T(8,128)(2,1)}, bf16[3,1152,2304]{2,1,0:T(8,128)(2,1)}) custom-call(bf16[9,96,2304]{2,1,0:T(8,128)(2,1)} %get-tuple-element.113.refs_0_, bf16[3,96,2304]{2,1,0:T(8,128)(2,1)} %get-tuple-element.114.refs_1_, ...), custom_call_target="tpu_custom_call" | custom-call | bytes 100000000 | tf_op jit(solution)/shard_map/stack_layers/pallas_call | solution.py:731
  1119.7 3.4 copy.19
  1123.1 1.4 copy.20
  (12 shorter events, 0.2 us)
Async XLA Ops:
  0.6 2.4 copy-start
  3.4 4.1 copy-start.2
  1119.7 3.4 copy-start.1
